TPU v7x, 8 devices: a whole 2x2x1 slice. The times are simulated.
8 devices in a mesh: dp: 1 (over z), sp: 8 (over y, x, core).
Axes of the slice: x: 2, y: 2, z: 1, core: 2. Of those that a mesh axis runs over, the one named last changes fastest.
Arguments:
- hidden_in: bfloat16 [8192, 1152], P(('dp', 'sp'))
- w_query: bfloat16 [1152, 4, 256], replicated
- w_key: bfloat16 [1152, 1, 256], replicated
- w_value: bfloat16 [1152, 1, 256], replicated
- w_out: bfloat16 [4, 256, 1152], replicated
- w_up: bfloat16 [1152, 6912], replicated
- w_down: bfloat16 [6912, 1152], replicated
- rel_bias: float32 [4, 1025], replicated
- glob_pos: int32 [256], P('dp')
Outputs:
- output 1: bfloat16 [8192, 1152], P(('dp', 'sp'))
- output 2: bfloat16 [256, 1152], P('dp')
All inputs are finite; a program needn't handle non-finite values.
Results may differ from a plain program's by a relative error of at most 0.00846168.
Values are sent between devices in bfloat16 or wider.
A program may use at most 1 GiB of HBM per device.

v0:
```python
import jax
import jax.numpy as jnp
from jax import lax
from jax.sharding import PartitionSpec as P


def three_blocks(ext, width):
    blocks = ext.reshape((ext.shape[0] // width, width) + ext.shape[1:])
    return jnp.concatenate([blocks[:-2], blocks[1:-1], blocks[2:]], axis=1)


def bias_tile(rel_bias, kv_heads):
    heads, span = rel_bias.shape
    width = (span - 1) // 2
    padded = jnp.pad(rel_bias, ((0, 0), (0, width)))
    tiled = jnp.tile(padded, (1, width))[:, : 3 * width * width]
    return tiled.reshape(kv_heads, heads // kv_heads, width, 3 * width)


def project(hidden_in, w_query, w_key, w_value):
    head = w_query.shape[2]
    queries = (jnp.einsum('td,dhe->the', hidden_in, w_query, preferred_element_type=jnp.float32) * head ** -0.5).astype(jnp.bfloat16)
    keys_loc = jnp.einsum('td,dge->tge', hidden_in, w_key, preferred_element_type=jnp.float32).astype(jnp.bfloat16)
    vals_loc = jnp.einsum('td,dge->tge', hidden_in, w_value, preferred_element_type=jnp.float32).astype(jnp.bfloat16)
    return queries, keys_loc, vals_loc


def window_attention(query_blk, key_win, val_win, key_ok, bias, key_glob, val_glob):
    width = query_blk.shape[1]
    row_idx = jnp.arange(width)[:, None]
    col_idx = jnp.arange(3 * width)[None, :]
    band = jnp.abs(col_idx - width - row_idx) <= width
    mask = band & key_ok[:, None, None, None, :]
    score_win = jnp.einsum('bqgrd,bkgd->bgrqk', query_blk, key_win, preferred_element_type=jnp.float32) + bias
    score_win = jnp.where(mask, score_win, -1e30)
    score_glob = jnp.einsum('bqgrd,ngd->bgrqn', query_blk, key_glob, preferred_element_type=jnp.float32)
    top = jnp.maximum(score_win.max(-1), score_glob.max(-1))[..., None]
    prob_win = jnp.exp(score_win - top)
    prob_glob = jnp.exp(score_glob - top)
    norm_sum = prob_win.sum(-1) + prob_glob.sum(-1)
    weighted = jnp.einsum('bgrqk,bkgd->bqgrd', prob_win.astype(jnp.bfloat16), val_win, preferred_element_type=jnp.float32)
    weighted = weighted + jnp.einsum('bgrqn,ngd->bqgrd', prob_glob.astype(jnp.bfloat16), val_glob, preferred_element_type=jnp.float32)
    return weighted / jnp.moveaxis(norm_sum, 3, 1)[..., None]


def global_partial(query_glob, keys_loc, vals_loc):
    scores = jnp.einsum('ngrd,tgd->ngrt', query_glob, keys_loc, preferred_element_type=jnp.float32)
    top = scores.max(-1)
    weights = jnp.exp(scores - top[..., None])
    weighted = jnp.einsum('ngrt,tgd->ngrd', weights.astype(jnp.bfloat16), vals_loc, preferred_element_type=jnp.float32)
    return top, weights.sum(-1), weighted


def finish_layer(hidden_in, attended, w_out, w_up, w_down):
    hidden = (hidden_in.astype(jnp.float32) + jnp.einsum('the,hed->td', attended, w_out, preferred_element_type=jnp.float32)).astype(jnp.bfloat16)
    upper = jax.nn.gelu(jnp.dot(hidden, w_up, preferred_element_type=jnp.float32)).astype(jnp.bfloat16)
    return (hidden.astype(jnp.float32) + jnp.dot(upper, w_down, preferred_element_type=jnp.float32)).astype(jnp.bfloat16)


def solution(mesh):
    sp_size = mesh.shape['sp']
    to_right = [(src, src + 1) for src in range(sp_size - 1)]
    to_left = [(src + 1, src) for src in range(sp_size - 1)]

    def shard_layer(hidden_in, w_query, w_key, w_value, w_out, w_up, w_down, rel_bias, glob_pos):
        rows = hidden_in.shape[0]
        heads, head = w_query.shape[1], w_query.shape[2]
        kv_heads = w_key.shape[1]
        group = heads // kv_heads
        width = (rel_bias.shape[1] - 1) // 2
        n_glob = glob_pos.shape[0]
        seq_len = rows * sp_size
        start = lax.axis_index('sp') * rows
        queries, keys_loc, vals_loc = project(hidden_in, w_query, w_key, w_value)
        owner = glob_pos[:, None] == (start + jnp.arange(rows))[None, :]
        pick = owner.astype(jnp.bfloat16)
        query_pick = jnp.einsum('nt,the->nhe', pick, queries, preferred_element_type=jnp.float32).astype(jnp.bfloat16)
        key_pick = jnp.einsum('nt,tge->nge', pick, keys_loc, preferred_element_type=jnp.float32).astype(jnp.bfloat16)
        val_pick = jnp.einsum('nt,tge->nge', pick, vals_loc, preferred_element_type=jnp.float32).astype(jnp.bfloat16)
        query_glob, key_glob, val_glob = lax.psum((query_pick, key_pick, val_pick), 'sp')
        keyval_loc = jnp.concatenate([keys_loc, vals_loc], axis=1)
        from_left = lax.ppermute(keyval_loc[rows - width:], 'sp', to_right)
        from_right = lax.ppermute(keyval_loc[:width], 'sp', to_left)
        keyval_ext = jnp.concatenate([from_left, keyval_loc, from_right], axis=0)
        ext_pos = start - width + jnp.arange(rows + 2 * width)
        is_glob_key = jnp.any(glob_pos[:, None] == ext_pos[None, :], axis=0)
        key_ok = (ext_pos >= 0) & (ext_pos < seq_len) & jnp.logical_not(is_glob_key)
        out_win = window_attention(
            queries.reshape(rows // width, width, kv_heads, group, head),
            three_blocks(keyval_ext[:, :kv_heads], width), three_blocks(keyval_ext[:, kv_heads:], width),
            three_blocks(key_ok, width), bias_tile(rel_bias, kv_heads), key_glob, val_glob)
        top, total, weighted = global_partial(query_glob.reshape(n_glob, kv_heads, group, head), keys_loc, vals_loc)
        best = lax.pmax(top, 'sp')
        rescale = jnp.exp(top - best)
        total, weighted = lax.psum((total * rescale, weighted * rescale[..., None]), 'sp')
        out_glob = (weighted / total[..., None]).astype(jnp.bfloat16).reshape(n_glob, heads, head)
        placed = jnp.einsum('nt,nhe->the', pick, out_glob, preferred_element_type=jnp.float32)
        is_glob_row = jnp.any(owner, axis=0)
        attended = jnp.where(is_glob_row[:, None, None], placed, out_win.reshape(rows, heads, head)).astype(jnp.bfloat16)
        y_out = finish_layer(hidden_in, attended, w_out, w_up, w_down)
        y_pick = jnp.einsum('nt,td->nd', pick, y_out, preferred_element_type=jnp.float32).astype(jnp.bfloat16)
        return y_out, lax.psum(y_pick, 'sp')

    return jax.shard_map(
        shard_layer, mesh=mesh,
        in_specs=(P(('dp', 'sp'), None), P(), P(), P(), P(), P(), P(), P(), P('dp')),
        out_specs=(P(('dp', 'sp'), None), P('dp', None)),
        check_vma=False)
```

profile of v0, /device:TPU:0, one launch (start us, length us, event | category | flops | bytes accessed | tf_op | source)
XLA Modules:
  0.0 347.3 jit_solution(13817347797109693115)
XLA Ops:
  7.2 0.0 copy-start
  7.2 0.0 all-reduce.10.cloned.1.call-start
  7.2 0.0 copy-start.16
  7.2 2.8 convolution_convert_fusion.1
  10.0 0.0 copy-done.16
  10.0 0.0 copy-done.17
  10.0 0.0 copy-start.13
  10.1 0.8 convolution_convert_fusion.2
  10.9 1.1 fusion.86
  12.0 3.5 %collective-permute-start = (bf16[512,2,256]{2,0,1:T(8,128)(2,1)}, bf16[512,2,256]{2,0,1:T(8,128)(2,1)}, u32[]{:S(2)}, u32[]{:S(2)}) collective-permute-start(bf16[512,2,256]{2,0,1:T(8,128)(2,1)} %get-tuple-element.11), channel_id=1, source_target_pairs={{0,1},{1,2},{2,3},{3,4},{4,5},{5,6},{6,7}} | collective-permute-start | bytes 1572872 | tf_op jit(solution)/shard_map/ppermute | solution.py:82
  15.5 1.3 collective-permute-start.1
  16.8 1.0 fusion.75
  17.8 1.0 fusion.78
  18.8 5.2 %multiply_convert_fusion = bf16[1024,4,256]{2,0,1:T(8,128)(2,1)S(1)} fusion(bf16[1152,4,256]{2,1,0:T(4,128)(2,1)} %param.10, bf16[1024,1152]{1,0:T(8,128)(2,1)} %param.9), kind=kOutput, calls=%fused_computation.32 | convolution fusion | flops 2418016256 | bytes 6815744 | tf_op jit(solution)/shard_map/td,dhe->the/dot_general | solution.py:22
  24.1 0.0 copy-start.4
  24.1 1.3 copy-done.4
  25.4 1.6 convolution_convert_fusion.3
  27.0 0.0 all-reduce.10.cloned.1.call-update
  27.0 0.6 all-reduce.6.cloned.1.call-start
  27.6 0.8 compare_reduce_fusion
  28.4 0.0 copy-done.9
  28.4 5.8 %tile.4 = f32[4,512,1537]{2,1,0:T(8,128)} broadcast(f32[4,1537]{1,0:T(4,128)S(1)} %pad.4), dimensions={0,2} | broadcast | bytes 12615696 | tf_op jit(solution)/shard_map/tile | solution.py:16
  34.1 20.2 %reshape.216 = f32[3147776]{0:T(1024)} reshape(f32[4,512,1537]{2,1,0:T(8,128)} %tile.4) | data formatting | bytes 25182208
  54.3 15.0 %tile.10 = f32[4,786944]{1,0:T(4,128)} reshape(f32[3147776]{0:T(1024)} %reshape.216) | data formatting | bytes 25182208 | tf_op jit(solution)/shard_map/tile | solution.py:16
  69.3 10.5 %slice.91 = f32[4,786432]{1,0:T(4,128)} slice(f32[4,786944]{1,0:T(4,128)} %tile.10), slice={[0:4], [0:786432]} | slice | bytes 25165824 | tf_op jit(solution)/shard_map/slice | solution.py:16
  79.9 13.2 %copy.75 = f32[1,4,512,1536]{3,2,1,0:T(8,128)} copy(f32[1,4,512,1536]{3,1,2,0:T(4,128)} %bitcast.203) | data formatting | bytes 25165824
  93.0 12.7 %copy.42 = f32[4,512,1536]{1,2,0:T(8,128)} copy(f32[4,512,1536]{2,1,0:T(8,128)} %bitcast.204) | data formatting | bytes 25165824 | tf_op jit(solution)/shard_map/add | solution.py:34
  105.7 0.4 compare_reduce_fusion.1
  106.1 1.8 abs_compare_fusion
  107.9 1.0 copy.39
  108.9 2.8 broadcast_and_fusion
  111.7 1.8 bitcast_reduce_fusion.1
  113.5 1.9 copy-done.2
  115.5 0.6 fusion.28
  116.0 25.9 %pmax.7 = f32[256,1,4]{0,2,1:T(4,128)S(1)} all-reduce(f32[256,1,4]{0,2,1:T(4,128)S(1)} %bitcast.218), channel_id=1, replica_groups=mesh['dp'=1,'sp'=8] {'sp'}, use_global_device_ids=true, to_apply=%region_3.0 | all-reduce | flops 1024 | bytes 8192 | tf_op jit(solution)/shard_map/pmax | solution.py:93
  141.9 3.9 %fusion.72 = f32[256,1,4,256]{0,3,2,1:T(8,128)} fusion(f32[1024,256,4]{1,0,2:T(8,128)} %copy-done.2, f32[256,4]{0,1:T(4,128)S(1)} %get-tuple-element.22, bf16[1024,256]{1,0:T(8,128)(2,1)S(1)} %convolution_convert_fusion.2, f32[256,4]{0,1:T(4,128)S(1)} %get-tuple-element.14), kind=kOutput, calls=%fused_computation.74 | convolution fusion | flops 539230208 | bytes 5775360 | tf_op jit(solution)/shard_map/ngrt,tgd->ngrd/dot_general | solution.py:50
  145.8 0.0 all-reduce.6.cloned.1.call-update
  145.8 0.0 all-reduce.8.cloned.1.call-start
  145.9 24.2 %psum.44 = f32[256,4]{0,1:T(4,128)} all-reduce(f32[256,4]{0,1:T(4,128)S(1)} %get-tuple-element.13), channel_id=1, replica_groups=mesh['dp'=1,'sp'=8] {'sp'}, use_global_device_ids=true, to_apply=%region_6.7 | all-reduce | flops 1024 | bytes 8192 | tf_op jit(solution)/shard_map/psum | solution.py:95
  170.1 4.3 %bitcast_reduce_fusion = (f32[2,4,512]{2,1,0:T(4,128)S(1)}, f32[256,2,512,4]{2,0,3,1:T(8,128)}) fusion(bf16[2,512,4,256]{3,1,0,2:T(8,128)(2,1)} %bitcast.205, bf16[256,256]{1,0:T(8,128)(2,1)S(1)} %copy-done.8), kind=kOutput, calls=%fused_computation.26 | convolution fusion | flops 537915392 | bytes 6438912 | tf_op jit(solution)/shard_map/bqgrd,ngd->bgrqn/dot_general | solution.py:36
  174.4 0.0 collective-permute-done
  174.4 0.0 collective-permute-done.1
  174.4 2.5 pad_maximum_fusion.6
  177.0 15.0 %fusion.11 = (f32[2,4,512]{2,1,0:T(4,128)S(1)}, f32[2,1536,512,4]{2,1,3,0:T(8,128)}) fusion(f32[4,512,1536]{1,2,0:T(8,128)} %copy.42, pred[2,512,1536]{1,2,0:T(8,128)(4,1)} %broadcast_and_fusion, bf16[2,512,4,256]{3,1,0,2:T(8,128)(2,1)} %bitcast.206, bf16[2,512,1,256]{3,1,0,2:T(8,128)(2,1)} %bitcast.214, bf16[2,512,1,256]{3,1,0,2:T(8,128)(2,1)S(1)} %bitcast.209, ...), kind=kOutput, calls=%fused_computation.14 | convolution fusion | flops 3244814336 | bytes 43008000 | tf_op jit(solution)/shard_map/bqgrd,bkgd->bgrqk/dot_general | solution.py:34
  192.0 3.0 fusion.30
  194.9 0.5 copy-done.1
  195.4 2.7 fusion.43
  198.1 0.0 copy-done.3
  198.1 13.9 %fusion.9 = f32[2,4,512]{2,1,0:T(4,128)S(1)} fusion(f32[2,1536,512,4]{2,1,3,0:T(8,128)} %get-tuple-element.19, f32[2,4,512]{2,1,0:T(4,128)S(1)} %max.11, f32[4,512,1536]{1,2,0:T(8,128)} %copy.42, pred[2,512,1536]{1,2,0:T(8,128)(4,1)S(1)} %copy-done.3), kind=kLoop, calls=%fused_computation.12 | loop fusion | flops 25161728 | bytes 39354368 | tf_op jit(solution)/shard_map/reduce_sum | solution.py:40
  212.0 0.0 copy-done.6
  212.0 1.0 copy.40
  213.0 0.2 copy.38
  213.3 17.2 %fusion.22 = bf16[2,512,1,4,256]{1,4,3,0,2:T(8,128)(2,1)} fusion(f32[256,2,4,512]{3,0,2,1:T(8,128)} %fusion.43, f32[2,1536,512,4]{2,1,3,0:T(8,128)} %get-tuple-element.19, f32[2,4,512]{2,1,0:T(4,128)S(1)} %max.11, f32[4,512,1536]{1,2,0:T(8,128)} %copy.42, pred[2,512,1536]{1,2,0:T(8,128)(4,1)} %broadcast_and_fusion, f32[2,512,4]{1,2,0:T(4,128)S(1)} %add_bitcast_fusion, ...), kind=kOutput, calls=%fused_computation.24 | convolution fusion | flops 3254255616 | bytes 47218688 | tf_op jit(solution)/shard_map/bgrqk,bkgd->bqgrd/dot_general | solution.py:41
  230.5 0.0 copy-start.14
  230.5 4.1 %copy.47 = bf16[2,512,1,4,256]{4,1,0,3,2:T(8,128)(2,1)} copy(bf16[2,512,1,4,256]{1,4,3,0,2:T(8,128)(2,1)} %fusion.22) | data formatting | bytes 4194304 | tf_op jit(solution)/shard_map/div | solution.py:43
  234.7 7.8 %fusion.21 = bf16[1024,1152]{1,0:T(8,128)(2,1)} fusion(bf16[1024,1152]{1,0:T(8,128)(2,1)} %param.9, bf16[4,256,1152]{2,1,0:T(8,128)(2,1)S(1)} %copy-done, bf16[1024,4,256]{2,0,1:T(8,128)(2,1)} %bitcast.215, pred[1024]{0:T(1024)(128)(4,1)S(1)} %copy-done.15, f32[256,1,4,256]{0,3,2,1:T(8,128)} %all-reduce.6.cloned.1.call-done, f32[256,4]{0,1:T(4,128)S(1)} %copy-done.12, ...), kind=kOutput, calls=%fused_computation.22 | convolution fusion | flops 2958426112 | bytes 10233856 | tf_op jit(solution)/shard_map/the,hed->td/dot_general | solution.py:55
  242.5 26.8 %fusion.149 = bf16[1024,6912]{1,0:T(8,128)(2,1)S(1)} fusion(bf16[1152,6912]{1,0:T(8,128)(2,1)} %param.14, bf16[1024,1152]{1,0:T(8,128)(2,1)} %fusion.21), kind=kOutput, calls=%fused_computation.8.clone.clone.clone.clone.clone.clone.1 | convolution fusion | flops 16371154944 | bytes 32440320 | tf_op jit(solution)/shard_map/dot_general | solution.py:56
  269.3 21.2 %fusion.25 = bf16[1024,1152]{1,0:T(8,128)(2,1)S(1)} fusion(bf16[6912,1152]{1,0:T(8,128)(2,1)} %param.15, bf16[1024,1152]{1,0:T(8,128)(2,1)S(1)} %copy-done.19, bf16[1024,6912]{1,0:T(8,128)(2,1)S(1)} %fusion.149), kind=kOutput, calls=%fused_computation.33 | convolution fusion | flops 16310992896 | bytes 34799616 | tf_op jit(solution)/shard_map/dot_general | solution.py:57
  290.6 0.0 copy-start.18
  290.6 1.4 copy-done.18
  292.0 1.7 convolution_convert_fusion
  293.7 0.0 all-reduce.8.cloned.1.call-update
  293.7 44.9 %all-reduce.8.cloned.1.call-done = bf16[256,1152]{1,0:T(8,128)(2,1)} async-done(((bf16[256,1152]{1,0:T(8,128)(2,1)}), bf16[256,1152]{1,0:T(8,128)(2,1)}) %all-reduce.8.cloned.1.call-update) | async-done | bytes 589840 | tf_op jit(solution)/shard_map/psum | solution.py:102
  338.6 1.9 copy.81
  (39 shorter events, 0.2 us)
Async XLA Ops:
  7.2 227.5 %copy-start = (bf16[4,256,1152]{2,1,0:T(8,128)(2,1)S(1)}, bf16[4,256,1152]{2,1,0:T(8,128)(2,1)}, u32[]{:S(2)}) copy-start(bf16[4,256,1152]{2,1,0:T(8,128)(2,1)} %param.13) | copy-start | bytes 7077892
  7.2 104.5 %all-reduce.10.cloned.1.call-start = ((), (), s32[]{:S(2)}) async-start(), calls=%async_computation.2 | async-start | bytes 1572864 | tf_op jit(solution)/shard_map/psum | solution.py:80
  7.2 2.8 copy-start.16
  7.2 2.8 copy-start.17
  10.0 6.8 %copy-start.13 = (s32[256]{0:T(256)S(1)}, s32[256]{0:T(256)}, u32[]{:S(2)}) copy-start(s32[256]{0:T(256)} %param.17) | copy-start | bytes 3076
  12.0 162.5 %collective-permute-start = (bf16[512,2,256]{2,0,1:T(8,128)(2,1)}, bf16[512,2,256]{2,0,1:T(8,128)(2,1)}, u32[]{:S(2)}, u32[]{:S(2)}) collective-permute-start(bf16[512,2,256]{2,0,1:T(8,128)(2,1)} %get-tuple-element.11), channel_id=1, source_target_pairs={{0,1},{1,2},{2,3},{3,4},{4,5},{5,6},{6,7}} | collective-permute-start | bytes 1572872 | tf_op jit(solution)/shard_map/ppermute | solution.py:82
  15.5 158.9 %collective-permute-start.1 = (bf16[512,2,256]{2,0,1:T(8,128)(2,1)}, bf16[512,2,256]{2,0,1:T(8,128)(2,1)}, u32[]{:S(2)}, u32[]{:S(2)}) collective-permute-start(bf16[512,2,256]{2,0,1:T(8,128)(2,1)} %get-tuple-element.12), channel_id=1, source_target_pairs={{1,0},{2,1},{3,2},{4,3},{5,4},{6,5},{7,6}} | collective-permute-start | bytes 1572872 | tf_op jit(solution)/shard_map/ppermute | solution.py:83
  16.8 10.8 %copy-start.10 = (s32[1024]{0:T(1024)}, s32[1024]{0:T(1024)S(1)}, u32[]{:S(2)}) copy-start(s32[1024]{0:T(1024)S(1)} %iota_add_fusion.2) | copy-start | bytes 12292
  24.1 1.3 copy-start.4
  25.4 3.0 copy-start.9
  27.0 207.6 %all-reduce.6.cloned.1.call-start = ((), (), s32[]{:S(2)}) async-start(), calls=%async_computation | async-start | bytes 2097152 | tf_op jit(solution)/shard_map/psum | solution.py:95
  113.5 1.9 copy-start.2
  116.0 54.1 %copy-start.8 = (bf16[256,256]{1,0:T(8,128)(2,1)S(1)}, bf16[256,256]{1,0:T(8,128)(2,1)}, u32[]{:S(2)}) copy-start(bf16[256,256]{1,0:T(8,128)(2,1)} %get-tuple-element.2) | copy-start | bytes 393220
  145.8 192.8 %all-reduce.8.cloned.1.call-start = ((), (), s32[]{:S(2)}) async-start(), calls=%async_computation.1 | async-start | bytes 1179648 | tf_op jit(solution)/shard_map/psum | solution.py:102
  177.0 18.0 %copy-start.7 = (bf16[256,256]{1,0:T(8,128)(2,1)S(1)}, bf16[256,256]{1,0:T(8,128)(2,1)}, u32[]{:S(2)}) copy-start(bf16[256,256]{1,0:T(8,128)(2,1)} %get-tuple-element.3) | copy-start | bytes 393220
  192.0 3.4 copy-start.1
  195.4 2.7 copy-start.3
  198.1 13.9 %copy-start.6 = (bf16[1024,1,256]{2,0,1:T(8,128)(2,1)S(1)}, bf16[1024,1,256]{2,0,1:T(8,128)(2,1)}, u32[]{:S(2)}) copy-start(bf16[1024,1,256]{2,0,1:T(8,128)(2,1)} %get-tuple-element.10) | copy-start | bytes 1572868
  198.1 14.9 %copy-start.5 = (bf16[1024,1,256]{2,0,1:T(8,128)(2,1)S(1)}, bf16[1024,1,256]{2,0,1:T(8,128)(2,1)}, u32[]{:S(2)}) copy-start(bf16[1024,1,256]{2,0,1:T(8,128)(2,1)} %get-tuple-element.5) | copy-start | bytes 1572868
  230.5 4.2 %copy-start.11 = (s32[1024]{0:T(1024)S(1)}, s32[1024]{0:T(1024)}, u32[]{:S(2)}) copy-start(s32[1024]{0:T(1024)} %copy-done.10) | copy-start | bytes 12292
  230.5 4.2 %copy-start.12 = (f32[256,4]{0,1:T(4,128)S(1)}, f32[256,4]{0,1:T(4,128)}, u32[]{:S(2)}) copy-start(f32[256,4]{0,1:T(4,128)} %psum.44) | copy-start | bytes 12292
  230.5 4.2 %copy-start.14 = (s32[256]{0:T(256)S(1)}, s32[256]{0:T(256)}, u32[]{:S(2)}) copy-start(s32[256]{0:T(256)} %param.17) | copy-start | bytes 3076
  230.5 4.2 %copy-start.15 = (pred[1024]{0:T(1024)(128)(4,1)S(1)}, pred[1024]{0:T(1024)(128)(4,1)}, u32[]{:S(2)}) copy-start(pred[1024]{0:T(1024)(128)(4,1)} %compare_reduce_fusion) | copy-start | bytes 3076
  242.5 26.8 %copy-start.19 = (bf16[1024,1152]{1,0:T(8,128)(2,1)S(1)}, bf16[1024,1152]{1,0:T(8,128)(2,1)}, u32[]{:S(2)}) copy-start(bf16[1024,1152]{1,0:T(8,128)(2,1)} %fusion.21) | copy-start | bytes 7077892
  290.6 1.4 copy-start.18
Sparse Core Ops, SparseCore 0:
  27.1 48.1 all-reduce.9
  146.0 47.1 all-reduce.5
  293.8 44.7 all-reduce.7
where the time goes:
time: 352 us; the launch traced here: 347 us
  matrix products  115 us (33%)
  local copies, waits for them, and re-layouts  90.8 us (26%)
  blocking collectives  50.1 us (14%)
  waiting for transfers between devices  45 us (13%)
  other arithmetic  26.8 us (8%)
  between operations  14.3 us (4%)
  starting transfers between devices  5.46 us (2%)
    psum x1, waiting for transfers between devices, shard_layer(): return (y_out, lax.psum(y_pick, 'sp'))  44.9 us
    unnamed x43, local copies, waits for them, and re-layouts  40.4 us
    dot_general x1, matrix products, finish_layer(): jnp.dot(hidden, w_up, preferred_element_type=jnp.float32)  26.8 us
    pmax x1, blocking collectives, shard_layer(): best = lax.pmax(top, 'sp')  25.9 us
    psum x1, blocking collectives, shard_layer(): lax.psum((total * rescale, weighted * rescale[..., None]), 'sp')  24.2 us
    dot_general x1, matrix products, finish_layer(): jnp.dot(upper, w_down, preferred_element_type=jnp.float32)  21.2 us
    another operation x2, local copies, waits for them, and re-layouts, bias_tile(): tiled = jnp.tile(padded, (1, width))[:, :3 * width * width]  20.8 us
    dot_general x1, matrix products, window_attention(): jnp.einsum('bgrqk,bkgd->bqgrd', prob_win.astype(jnp.bfloat16), val_win, p...  17.2 us
  transfers between devices with their start and end apart: 5, of which 1 were waited for; matrix products, arithmetic and copies ran while one was open for 47% of the time, Pallas kernels for 0%

commit v1 on v0

v1 whole, which is shorter than its diff:
```python
import functools
import math

import jax
import jax.numpy as jnp
from jax import lax
from jax.experimental import pallas as pl
from jax.experimental.pallas import tpu as pltpu
from jax.sharding import PartitionSpec as P

BF16 = jnp.bfloat16
F32 = jnp.float32
NEG = -math.inf
BLK = 256


def mm(a, b):
    return jnp.dot(a, b, preferred_element_type=F32)


def mm_nt(a, b):
    return lax.dot_general(a, b, (((1,), (1,)), ((), ())), preferred_element_type=F32)


def remote(src, dst, send, recv, dev):
    return pltpu.make_async_remote_copy(
        src_ref=src, dst_ref=dst, send_sem=send, recv_sem=recv,
        device_id={'sp': dev}, device_id_type=pl.DeviceIdType.MESH)


def entry_barrier(me, n_dev):
    barrier = pltpu.get_barrier_semaphore()
    for k in range(1, n_dev):
        pl.semaphore_signal(barrier, inc=1, device_id={'sp': lax.rem(me + k, n_dev)}, device_id_type=pl.DeviceIdType.MESH)
    pl.semaphore_wait(barrier, n_dev - 1)


def to_column(row):
    n = row.shape[1]
    wide = jnp.broadcast_to(row.astype(F32), (n, n))
    diag = lax.broadcasted_iota(jnp.int32, (n, n), 0) == lax.broadcasted_iota(jnp.int32, (n, n), 1)
    return jnp.sum(jnp.where(diag, wide, 0.0), axis=1, keepdims=True).astype(jnp.int32)


def front_kernel(n_dev, heads, width,
                 x_hbm, wq_hbm, wk_hbm, wv_hbm, wo_hbm, rb_ref, gp_ref, hid_ref,
                 x_s, wq_s, wk_s, wv_s, wo_s, q_s, kv_s, kvl_s, kvr_s, bias_s, row_s, mask_s,
                 xg_send, xg_recv, xg_all, qg_s, kvg_s, o_s, m_s, l_s, att_s, rs_send, rs_recv,
                 in_sem, x1_send, x1_recv, x2_send, x2_recv, halo_send, halo_recv, rs_ssem, rs_rsem):
    rows, dim = x_s.shape
    head = wk_s.shape[1]
    n_glob = gp_ref.shape[1]
    per = n_glob // n_dev
    n_blk = rows // BLK
    ext = BLK + 2 * width
    me = lax.axis_index('sp')
    start = me * rows

    loads = [pltpu.make_async_copy(src, dst, in_sem.at[i]) for i, (src, dst) in enumerate(
        [(x_hbm, x_s), (wk_hbm, wk_s), (wv_hbm, wv_s), (wq_hbm, wq_s), (wo_hbm, wo_s)])]
    for c in loads:
        c.start()
    entry_barrier(me, n_dev)

    gp_row = gp_ref[...]
    gp_col = to_column(gp_row)
    loads[0].wait()
    x = x_s[...]

    own = gp_col == start + lax.broadcasted_iota(jnp.int32, (n_glob, rows), 1)
    xg_send[...] = mm(own.astype(F32).astype(BF16), x).astype(BF16)
    x1 = []
    for k in range(1, n_dev):
        peer = lax.rem(me + k, n_dev)
        c = remote(xg_send.at[pl.ds(peer * per, per)], xg_recv.at[k], x1_send.at[k], x1_recv.at[k], peer)
        c.start()
        x1.append(c)

    loads[1].wait()
    loads[2].wait()
    kv_s[:, :head] = mm(x, wk_s[...]).astype(BF16)
    kv_s[:, head:] = mm(x, wv_s[...]).astype(BF16)

    to_right = remote(kv_s.at[pl.ds(rows - width, width)], kvl_s, halo_send.at[0], halo_recv.at[0], lax.rem(me + 1, n_dev))
    to_left = remote(kv_s.at[pl.ds(0, width)], kvr_s, halo_send.at[1], halo_recv.at[1], lax.rem(me + n_dev - 1, n_dev))

    @pl.when(me < n_dev - 1)
    def _():
        to_right.start()

    @pl.when(me > 0)
    def _():
        to_left.start()

    @pl.when(me == 0)
    def _():
        kvl_s[...] = jnp.zeros_like(kvl_s)

    @pl.when(me == n_dev - 1)
    def _():
        kvr_s[...] = jnp.zeros_like(kvr_s)

    loads[3].wait()
    for h in range(heads):
        qh = (mm(x, wq_s[:, h * head:(h + 1) * head]) * head ** -0.5).astype(BF16)
        for b in range(n_blk):
            q_s[b, h * BLK:(h + 1) * BLK, :] = qh[b * BLK:(b + 1) * BLK]

    pos = start - width + lax.broadcasted_iota(jnp.int32, (1, rows + 2 * width), 1)
    hit = jnp.max((gp_col == pos).astype(F32), axis=0, keepdims=True) > 0.0
    bad = hit | (pos < 0) | (pos >= rows * n_dev)
    mask_s[...] = jnp.broadcast_to(jnp.where(bad, NEG, 0.0), mask_s.shape)

    row_s[...] = jnp.full(row_s.shape, NEG, F32)
    row_s[:heads, :2 * width] = rb_ref[:, :2 * width]
    last = jnp.broadcast_to(rb_ref[:, 2 * width:], (heads, 128))
    row_s[:heads, 2 * width:2 * width + 128] = jnp.where(lax.broadcasted_iota(jnp.int32, (heads, 128), 1) == 0, last, NEG)
    for h in range(heads):
        wide = jnp.broadcast_to(row_s[h:h + 1, :], (BLK, ext))
        bias_s[h * BLK:(h + 1) * BLK, :] = pltpu.roll(wide, 0, 1, stride=1, stride_axis=0)

    def local_part(b):
        lo = max(0, b * BLK - width)
        hi = min(rows, (b + 1) * BLK + width)
        c0 = lo - b * BLK + width
        for h in range(heads):
            rs = slice(h * BLK, (h + 1) * BLK)
            s = mm_nt(q_s[b, rs, :], kv_s[lo:hi, :head])
            s = s + bias_s[rs, c0:c0 + hi - lo] + mask_s[0:1, width + lo:width + hi]
            top = jnp.max(s, axis=1, keepdims=True)
            p = jnp.exp(s - top)
            l_s[b, rs, :] = jnp.broadcast_to(jnp.sum(p, axis=1, keepdims=True), (BLK, 128))
            m_s[b, rs, :] = jnp.broadcast_to(top, (BLK, 128))
            o_s[b, rs, :] = mm(p.astype(BF16), kv_s[lo:hi, head:])

    def far_part(b):
        if b * BLK < width:
            ref, lo, hi, c0 = kvl_s, b * BLK, width, 0
            mask0 = lo
        else:
            ref, lo, hi = kvr_s, 0, (b + 1) * BLK + width - rows
            c0 = ext - hi
            mask0 = width + rows
        for h in range(heads):
            rs = slice(h * BLK, (h + 1) * BLK)
            q = q_s[b, rs, :]
            sw = mm_nt(q, ref[lo:hi, :head])
            sw = sw + bias_s[rs, c0:c0 + hi - lo] + mask_s[0:1, mask0:mask0 + hi - lo]
            sg = mm_nt(q, kvg_s[:, :head])
            m1 = m_s[b, rs, 0:1]
            top = jnp.maximum(m1, jnp.maximum(jnp.max(sw, axis=1, keepdims=True), jnp.max(sg, axis=1, keepdims=True)))
            pw = jnp.exp(sw - top)
            pg = jnp.exp(sg - top)
            fac = jnp.exp(m1 - top)
            tot = l_s[b, rs, 0:1] * fac + jnp.sum(pw, axis=1, keepdims=True) + jnp.sum(pg, axis=1, keepdims=True)
            o = o_s[b, rs, :] * fac + mm(pw.astype(BF16), ref[lo:hi, head:]) + mm(pg.astype(BF16), kvg_s[:, head:])
            att_s[b * BLK:(b + 1) * BLK, h * head:(h + 1) * head] = (o / tot).astype(BF16)

    local_part(0)
    local_part(1)

    for c in x1:
        c.wait_recv()
    acc = xg_send[pl.ds(me * per, per), :].astype(F32)
    for k in range(1, n_dev):
        acc = acc + xg_recv[k].astype(F32)
    xg_all[pl.ds(me * per, per), :] = acc.astype(BF16)
    x2 = []
    for k in range(1, n_dev):
        peer = lax.rem(me + k, n_dev)
        mine = xg_all.at[pl.ds(me * per, per)]
        c = remote(mine, mine, x2_send.at[k], x2_recv.at[k], peer)
        c.start()
        x2.append(c)

    local_part(2)
    local_part(3)

    for k in range(1, n_dev):
        src = lax.rem(me + n_dev - k, n_dev)
        got = xg_all.at[pl.ds(src * per, per)]
        remote(got, got, x2_send.at[k], x2_recv.at[k], src).wait_recv()
    xg = xg_all[...]
    kvg_s[:, :head] = mm(xg, wk_s[...]).astype(BF16)
    kvg_s[:, head:] = mm(xg, wv_s[...]).astype(BF16)
    for h in range(heads):
        qh = (mm(xg, wq_s[:, h * head:(h + 1) * head]) * head ** -0.5).astype(BF16)
        for j in range(n_dev):
            at = (j * heads + h) * per
            qg_s[at:at + per, :] = qh[j * per:(j + 1) * per]

    slab = heads * per
    for r in range(0, n_dev * slab, BLK):
        s = mm_nt(qg_s[r:r + BLK, :], kv_s[:, :head])
        top = jnp.max(s, axis=1, keepdims=True)
        p = jnp.exp(s - top)
        tot = jnp.sum(p, axis=1, keepdims=True)
        rs_send[r:r + BLK, :head] = mm(p.astype(BF16), kv_s[:, head:])
        lane = lax.broadcasted_iota(jnp.int32, (BLK, 128), 1)
        rs_send[r:r + BLK, head:] = jnp.where(lane < 64, top, tot)
    rs = []
    for k in range(1, n_dev):
        peer = lax.rem(me + k, n_dev)
        c = remote(rs_send.at[pl.ds(peer * slab, slab)], rs_recv.at[k], rs_ssem.at[k], rs_rsem.at[k], peer)
        c.start()
        rs.append(c)

    @pl.when(me > 0)
    def _():
        to_right.wait_recv()

    @pl.when(me < n_dev - 1)
    def _():
        to_left.wait_recv()

    for b in range(n_blk):
        far_part(b)

    loads[4].wait()
    for b in range(n_blk):
        r = slice(b * BLK, (b + 1) * BLK)
        hid_ref[r, :] = (x_s[r, :].astype(F32) + mm(att_s[r, :], wo_s[...])).astype(BF16)

    for c in rs:
        c.wait_recv()
    rs_recv[0] = rs_send[pl.ds(me * slab, slab), :]
    top = rs_recv[0, :, head:head + 1]
    for k in range(1, n_dev):
        top = jnp.maximum(top, rs_recv[k, :, head:head + 1])
    tot = jnp.zeros((slab, 1), F32)
    o = jnp.zeros((slab, head), F32)
    for k in range(n_dev):
        fac = jnp.exp(rs_recv[k, :, head:head + 1] - top)
        tot = tot + rs_recv[k, :, head + 64:head + 65] * fac
        o = o + rs_recv[k, :, :head] * fac
    o = (o / tot).astype(BF16)
    hg = xg_all[pl.ds(me * per, per), :].astype(F32)
    for h in range(heads):
        hg = hg + mm(o[h * per:(h + 1) * per], wo_s[h * head:(h + 1) * head, :])
    hid_ref[rows:, :] = hg.astype(BF16)

    for c in x1 + x2 + rs:
        c.wait_send()

    @pl.when(me < n_dev - 1)
    def _():
        to_right.wait_send()

    @pl.when(me > 0)
    def _():
        to_left.wait_send()


def front(x, wq, wk, wv, wo, rel_bias, gp, n_dev, heads):
    rows, dim = x.shape
    head = wk.shape[1]
    width = (rel_bias.shape[1] - 1) // 2
    n_glob = gp.shape[1]
    per = n_glob // n_dev
    n_blk = rows // BLK
    slab = heads * per
    any_spec = pl.BlockSpec(memory_space=pl.ANY)
    vmem_spec = pl.BlockSpec(memory_space=pltpu.VMEM)
    dma = pltpu.SemaphoreType.DMA
    return pl.pallas_call(
        functools.partial(front_kernel, n_dev, heads, width),
        name='front',
        out_shape=jax.ShapeDtypeStruct((rows + per, dim), BF16),
        in_specs=[any_spec] * 5 + [vmem_spec] * 2,
        out_specs=vmem_spec,
        scratch_shapes=[
            pltpu.VMEM(x.shape, BF16), pltpu.VMEM(wq.shape, BF16), pltpu.VMEM(wk.shape, BF16),
            pltpu.VMEM(wv.shape, BF16), pltpu.VMEM(wo.shape, BF16),
            pltpu.VMEM((n_blk, heads * BLK, head), BF16),
            pltpu.VMEM((rows, 2 * head), BF16), pltpu.VMEM((width, 2 * head), BF16), pltpu.VMEM((width, 2 * head), BF16),
            pltpu.VMEM((heads * BLK, BLK + 2 * width), F32), pltpu.VMEM((8, BLK + 2 * width), F32),
            pltpu.VMEM((8, rows + 2 * width), F32),
            pltpu.VMEM((n_glob, dim), BF16), pltpu.VMEM((n_dev, per, dim), BF16), pltpu.VMEM((n_glob, dim), BF16),
            pltpu.VMEM((n_dev * slab, head), BF16), pltpu.VMEM((n_glob, 2 * head), BF16),
            pltpu.VMEM((n_blk, heads * BLK, head), F32), pltpu.VMEM((n_blk, heads * BLK, 128), F32),
            pltpu.VMEM((n_blk, heads * BLK, 128), F32),
            pltpu.VMEM((rows, heads * head), BF16),
            pltpu.VMEM((n_dev * slab, head + 128), F32), pltpu.VMEM((n_dev, slab, head + 128), F32),
            dma((5,)), dma((n_dev,)), dma((n_dev,)), dma((n_dev,)), dma((n_dev,)), dma((2,)), dma((2,)), dma((n_dev,)), dma((n_dev,)),
        ],
        compiler_params=pltpu.CompilerParams(collective_id=0, has_side_effects=True, vmem_limit_bytes=62 << 20),
    )(x, wq, wk, wv, wo, rel_bias, gp)


def ffn_kernel(n_dev, rows, hid_ref, w1_ref, w2_ref, gp_ref, y_ref, yg_ref, acc_s, send_s, yg_s, u_s, ssem, rsem):
    step = pl.program_id(0)
    total = hid_ref.shape[0]
    n_glob = gp_ref.shape[1]
    per = n_glob // n_dev
    me = lax.axis_index('sp')
    tile = w1_ref.shape[1]

    @pl.when(step == 0)
    def _():
        entry_barrier(me, n_dev)
        acc_s[...] = hid_ref[...].astype(F32)

    for c in range(0, tile, BLK):
        u_s[:, c:c + BLK] = jax.nn.gelu(mm(hid_ref[...], w1_ref[:, c:c + BLK]), approximate=True).astype(BF16)
    acc_s[...] += mm(u_s[...], w2_ref[...])

    @pl.when(step == pl.num_programs(0) - 1)
    def _():
        send_s[...] = acc_s[rows:, :].astype(BF16)
        copies = []
        for k in range(1, n_dev):
            peer = lax.rem(me + k, n_dev)
            c = remote(send_s, yg_s.at[pl.ds(me * per, per)], ssem.at[k], rsem.at[k], peer)
            c.start()
            copies.append(c)
        yg_s[pl.ds(me * per, per), :] = send_s[...]
        for k in range(1, n_dev):
            src = lax.rem(me + n_dev - k, n_dev)
            remote(send_s, yg_s.at[pl.ds(src * per, per)], ssem.at[k], rsem.at[k], src).wait_recv()
        yg_ref[...] = yg_s[...]
        gp = gp_ref[...]
        for r in range(0, rows, BLK):
            hit = gp == me * rows + r + lax.broadcasted_iota(jnp.int32, (BLK, n_glob), 0)
            sel = hit.astype(F32)
            placed = mm(sel.astype(BF16), yg_s[...])
            is_glob = jnp.max(sel, axis=1, keepdims=True) > 0.0
            y_ref[r:r + BLK, :] = jnp.where(is_glob, placed, acc_s[r:r + BLK, :]).astype(BF16)
        for c in copies:
            c.wait_send()


def ffn(hid, w1, w2, gp, rows, n_dev, tile):
    total, dim = hid.shape
    wide = w1.shape[1]
    n_glob = gp.shape[1]
    dma = pltpu.SemaphoreType.DMA
    return pl.pallas_call(
        functools.partial(ffn_kernel, n_dev, rows),
        name='ffn',
        grid=(wide // tile,),
        out_shape=(jax.ShapeDtypeStruct((rows, dim), BF16), jax.ShapeDtypeStruct((n_glob, dim), BF16)),
        in_specs=[pl.BlockSpec((total, dim), lambda i: (0, 0)), pl.BlockSpec((dim, tile), lambda i: (0, i)),
                  pl.BlockSpec((tile, dim), lambda i: (i, 0)), pl.BlockSpec((1, n_glob), lambda i: (0, 0))],
        out_specs=(pl.BlockSpec(memory_space=pltpu.VMEM), pl.BlockSpec(memory_space=pltpu.VMEM)),
        scratch_shapes=[pltpu.VMEM((total, dim), F32), pltpu.VMEM((n_glob // n_dev, dim), BF16),
                        pltpu.VMEM((n_glob, dim), BF16), pltpu.VMEM((total, tile), BF16), dma((n_dev,)), dma((n_dev,))],
        compiler_params=pltpu.CompilerParams(
            dimension_semantics=('arbitrary',), collective_id=1, has_side_effects=True, vmem_limit_bytes=60 << 20),
    )(hid, w1, w2, gp)


def solution(mesh):
    n_dev = mesh.shape['sp']

    def shard_layer(hidden_in, w_query, w_key, w_value, w_out, w_up, w_down, rel_bias, glob_pos):
        rows, dim = hidden_in.shape
        heads, head = w_query.shape[1], w_query.shape[2]
        gp = glob_pos.reshape(1, -1)
        hid = front(hidden_in, w_query.reshape(dim, heads * head), w_key.reshape(dim, head), w_value.reshape(dim, head),
                    w_out.reshape(heads * head, dim), rel_bias, gp, n_dev, heads)
        return ffn(hid, w_up, w_down, gp, rows, n_dev, 768)

    return jax.shard_map(
        shard_layer, mesh=mesh,
        in_specs=(P(('dp', 'sp'), None), P(), P(), P(), P(), P(), P(), P(), P('dp')),
        out_specs=(P(('dp', 'sp'), None), P('dp', None)),
        check_vma=False)
```

time: 352 us -> 126 us (0.36); the launches traced: 347 us -> 126 us
  Pallas kernels: 0 us -> 118 us
  matrix products: 115 us -> 0 us
  local copies, waits for them, and re-layouts: 90.8 us -> 7.76 us
  blocking collectives: 50.1 us -> 0 us
  waiting for transfers between devices: 45 us -> 0 us
  other arithmetic: 26.8 us -> 0 us
  between operations: 14.3 us -> 0.66 us
  starting transfers between devices: 5.46 us -> 0 us
    pallas_call x0 -> x2, Pallas kernels: none -> 118 us  [the longest x1 64.8 us: ffn(): pl.pallas_call(functools.partial(ffn_kernel, n_dev, rows), name='ffn', gr...]
    dot_general x16 -> x0, matrix products: 115 us -> none  [the longest x1 26.8 us: finish_layer(): jnp.dot(hidden, w_up, preferred_element_type=jnp.float32)]
    psum x3 -> x0, waiting for transfers between devices: 44.9 us -> none  [the longest x1 44.9 us: shard_layer(): return (y_out, lax.psum(y_pick, 'sp'))]
    unnamed x43 -> x5, local copies, waits for them, and re-layouts: 40.4 us -> 7.76 us
    pmax x1 -> x0, blocking collectives: 25.9 us -> none  [shard_layer(): best = lax.pmax(top, 'sp')]
    psum x1 -> x0, blocking collectives: 24.2 us -> none  [shard_layer(): lax.psum((total * rescale, weighted * rescale[..., None]), 'sp')]
    another operation x2 -> x0, local copies, waits for them, and re-layouts: 20.8 us -> none  [bias_tile(): tiled = jnp.tile(padded, (1, width))[:, :3 * width * width]]
    reduce_sum x3 -> x0, other arithmetic: 17.4 us -> none  [the longest x2 16.8 us: window_attention(): norm_sum = prob_win.sum(-1) + prob_glob.sum(-1)]
  transfers between devices with their start and end apart: 5 -> 0, of which waited for: 1 -> 0; matrix products, arithmetic and copies ran while one was open for 47% -> 0% of each run, Pallas kernels for 0% -> 0%
where the time goes in v1:
time: 126 us
  Pallas kernels  118 us (94%)
  local copies, waits for them, and re-layouts  7.76 us (6%)
    pallas_call x1, Pallas kernels, ffn(): pl.pallas_call(functools.partial(ffn_kernel, n_dev, rows), name='ffn', gr...  64.8 us
    pallas_call x1, Pallas kernels, front(): pl.pallas_call(functools.partial(front_kernel, n_dev, heads, width), name...  53 us
    unnamed x5, local copies, waits for them, and re-layouts  7.76 us

profile of v1, /device:TPU:0, one launch (start us, length us, event | category | flops | bytes accessed | tf_op | source)
XLA Modules:
  0.0 126.2 jit_solution(11595589244176512215)
XLA Ops:
  0.6 3.6 %copy.11 = bf16[144,8,4,256]{3,1,2,0:T(8,128)(2,1)} copy(bf16[144,8,4,256]{3,2,1,0:T(4,128)(2,1)} %bitcast.7) | data formatting | bytes 4718592
  4.3 53.0 %front.1.hid_ref = bf16[1056,1152]{1,0:T(8,128)(2,1)} custom-call(bf16[1024,1152]{1,0:T(8,128)(2,1)} %x_hbm.1, bf16[1152,1024]{1,0:T(8,128)(2,1)} %bitcast.6, bf16[1152,256]{1,0:T(8,128)(2,1)} %bitcast.9, bf16[1152,256]{1,0:T(8,128)(2,1)} %bitcast.10, bf16[1024,1152]{1,0:T(8,128)(2,1)} %bitcast.8, f32[4,1025]{1,0:T(4,128)} %rb_ref.1, s32[1,256]{1,0:T(1,128)} %bitcast.11), custom_call_target="tpu_custom_call" | custom-call | tf_op jit(solution)/shard_map/front/pallas_call | solution.py:265
  57.3 64.8 %ffn.1 = (bf16[1024,1152]{1,0:T(8,128)(2,1)}, bf16[256,1152]{1,0:T(8,128)(2,1)}) custom-call(bf16[1056,1152]{1,0:T(8,128)(2,1)} %front.1.hid_ref, bf16[1152,6912]{1,0:T(8,128)(2,1)} %w1_ref.1, bf16[6912,1152]{1,0:T(8,128)(2,1)} %w2_ref.1, s32[1,256]{1,0:T(1,128)} %bitcast.12), custom_call_target="tpu_custom_call" | custom-call | tf_op jit(solution)/shard_map/ffn/pallas_call | solution.py:337
  122.0 0.0 copy-start
  122.1 3.3 %copy.14 = bf16[1024,1152]{1,0:T(8,128)(2,1)} copy(bf16[1024,1152]{1,0:T(8,128)(2,1)} %get-tuple-element.4) | data formatting | bytes 4718592
  125.4 0.0 copy-done
  125.4 0.8 copy.15
Async XLA Ops:
  122.0 3.3 %copy-start = (bf16[256,1152]{1,0:T(8,128)(2,1)S(1)}, bf16[256,1152]{1,0:T(8,128)(2,1)}, u32[]{:S(2)}) copy-start(bf16[256,1152]{1,0:T(8,128)(2,1)} %get-tuple-element.5) | copy-start | bytes 1769476

commit v2 on v1

v2 whole, which is shorter than its diff:
```python
import functools
import math

import jax
import jax.numpy as jnp
from jax import lax
from jax.experimental import pallas as pl
from jax.experimental.pallas import tpu as pltpu
from jax.sharding import PartitionSpec as P

BF16 = jnp.bfloat16
F32 = jnp.float32
NEG = -math.inf
BLK = 256


def mm(a, b):
    return jnp.dot(a, b, preferred_element_type=F32)


def mm_nt(a, b):
    return lax.dot_general(a, b, (((1,), (1,)), ((), ())), preferred_element_type=F32)


def remote(src, dst, send, recv, dev):
    return pltpu.make_async_remote_copy(
        src_ref=src, dst_ref=dst, send_sem=send, recv_sem=recv,
        device_id={'sp': dev}, device_id_type=pl.DeviceIdType.MESH)


def entry_barrier(me, n_dev):
    barrier = pltpu.get_barrier_semaphore()
    for k in range(1, n_dev):
        pl.semaphore_signal(barrier, inc=1, device_id={'sp': lax.rem(me + k, n_dev)}, device_id_type=pl.DeviceIdType.MESH)
    pl.semaphore_wait(barrier, n_dev - 1)


def diagonal(n):
    return lax.broadcasted_iota(jnp.int32, (n, n), 0) == lax.broadcasted_iota(jnp.int32, (n, n), 1)


def row_to_column(row):
    n = row.shape[1]
    return jnp.sum(jnp.where(diagonal(n), jnp.broadcast_to(row, (n, n)), 0.0), axis=1, keepdims=True)


def column_to_row(col):
    n = col.shape[0]
    return jnp.sum(jnp.where(diagonal(n), jnp.broadcast_to(col, (n, n)), 0.0), axis=0, keepdims=True)


def front_kernel(n_dev, heads, width,
                 x_hbm, wq_hbm, wk_hbm, wv_hbm, wo_hbm, rb_ref, gp_ref, hid_ref,
                 x_s, wq_s, wk_s, wv_s, wo_s, q_s, kv_s, halo_s, bias_s, row_s, mask_s,
                 xg_send, xp_recv, xh_s, xa_recv, xh2_s, xb_recv, xg_all, qg_s, kvg_s, o_s, m_s, l_s, att_s,
                 rs_send, rs_recv, st_send, st_recv,
                 in_sem, x_ssem, x_rsem, halo_send, halo_recv, rs_ssem, rs_rsem, st_ssem, st_rsem):
    rows, dim = x_s.shape
    head = wk_s.shape[1]
    n_glob = gp_ref.shape[1]
    per = n_glob // n_dev
    n_blk = rows // BLK
    ext = BLK + 2 * width
    me = lax.axis_index('sp')
    start = me * rows
    core = lax.rem(me, 2)
    chip = me // 2
    partner = me + 1 - 2 * core
    x_peer = 2 * (chip + 1 - 2 * lax.rem(chip, 2)) + core
    y_peer = 2 * lax.rem(chip + 2, 4) + core
    half = n_glob // 2
    quart = n_glob // 4

    loads = [pltpu.make_async_copy(src, dst, in_sem.at[i]) for i, (src, dst) in enumerate(
        [(x_hbm, x_s), (wk_hbm, wk_s), (wv_hbm, wv_s), (wq_hbm, wq_s), (wo_hbm, wo_s)])]
    for c in loads:
        c.start()
    entry_barrier(me, n_dev)

    gp_row = gp_ref[...]
    gp_col = row_to_column(gp_row.astype(F32)).astype(jnp.int32)
    loads[0].wait()
    x = x_s[...]

    own = gp_col == start + lax.broadcasted_iota(jnp.int32, (n_glob, rows), 1)
    xg_send[...] = mm(own.astype(F32).astype(BF16), x).astype(BF16)
    pair = remote(xg_send.at[pl.ds((1 - core) * half, half)], xp_recv, x_ssem.at[0], x_rsem.at[0], partner)
    pair.start()

    loads[1].wait()
    loads[2].wait()
    kv_s[:, :head] = mm(x, wk_s[...]).astype(BF16)
    kv_s[:, head:] = mm(x, wv_s[...]).astype(BF16)

    near, far = 1 - core, core
    has_far = (me > 0) & (me < n_dev - 1)
    to_near = remote(kv_s.at[pl.ds(near * width, width)], halo_s.at[core], halo_send.at[0], halo_recv.at[0], partner)
    to_far = remote(kv_s.at[pl.ds(far * width, width)], halo_s.at[1 - core], halo_send.at[1], halo_recv.at[1],
                    lax.rem(me + n_dev - 1 + 2 * core, n_dev))
    to_near.start()

    pair.wait_recv()
    xh_s[...] = (xg_send[pl.ds(core * half, half), :].astype(F32) + xp_recv[...].astype(F32)).astype(BF16)
    swap = [remote(xh_s.at[pl.ds(0, quart)], xa_recv.at[0], x_ssem.at[1], x_rsem.at[1], x_peer),
            remote(xh_s.at[pl.ds(quart, quart)], xa_recv.at[1], x_ssem.at[2], x_rsem.at[2], y_peer)]
    for c in swap:
        c.start()

    loads[3].wait()
    for h in range(heads):
        qh = (mm(x, wq_s[:, h * head:(h + 1) * head]) * head ** -0.5).astype(BF16)
        for b in range(n_blk):
            q_s[b, h * BLK:(h + 1) * BLK, :] = qh[b * BLK:(b + 1) * BLK]

    pos = start - width + lax.broadcasted_iota(jnp.int32, (1, rows + 2 * width), 1)
    hit = jnp.max((gp_col == pos).astype(F32), axis=0, keepdims=True) > 0.0
    bad = hit | (pos < 0) | (pos >= rows * n_dev)
    mask_s[...] = jnp.broadcast_to(jnp.where(bad, NEG, 0.0), mask_s.shape)

    row_s[...] = jnp.full(row_s.shape, NEG, F32)
    row_s[:heads, :2 * width] = rb_ref[:, :2 * width]
    last = jnp.broadcast_to(rb_ref[:, 2 * width:], (heads, 128))
    row_s[:heads, 2 * width:2 * width + 128] = jnp.where(lax.broadcasted_iota(jnp.int32, (heads, 128), 1) == 0, last, NEG)
    for h in range(heads):
        wide = jnp.broadcast_to(row_s[h:h + 1, :], (BLK, ext))
        bias_s[h * BLK:(h + 1) * BLK, :] = pltpu.roll(wide, 0, 1, stride=1, stride_axis=0)

    def local_part(b):
        lo = max(0, b * BLK - width)
        hi = min(rows, (b + 1) * BLK + width)
        c0 = lo - b * BLK + width
        for h in range(heads):
            rs = slice(h * BLK, (h + 1) * BLK)
            s = mm_nt(q_s[b, rs, :], kv_s[lo:hi, :head])
            s = s + bias_s[rs, c0:c0 + hi - lo] + mask_s[0:1, width + lo:width + hi]
            top = jnp.max(s, axis=1, keepdims=True)
            p = jnp.exp(s - top)
            l_s[b, rs, :] = jnp.broadcast_to(jnp.sum(p, axis=1, keepdims=True), (BLK, 128))
            m_s[b, rs, :] = jnp.broadcast_to(top, (BLK, 128))
            o_s[b, rs, :] = mm(p.astype(BF16), kv_s[lo:hi, head:])

    def far_part(side, n_keys):
        if n_keys == width:
            b, key0 = side * (n_blk - 1), 0
            mask0 = side * (width + rows)
        else:
            b, key0 = 1 + side * (n_blk - 3), (1 - side) * BLK
            mask0 = side * (width + rows) + key0
        c0 = side * (ext - n_keys)
        keys = pl.ds(pl.multiple_of(key0, BLK), n_keys)
        for h in range(heads):
            rs = slice(h * BLK, (h + 1) * BLK)
            q = q_s[b, rs, :]
            sw = mm_nt(q, halo_s[side, keys, :head])
            sw = sw + bias_s[rs, pl.ds(pl.multiple_of(c0, BLK), n_keys)] + mask_s[0:1, pl.ds(pl.multiple_of(mask0, BLK), n_keys)]
            sg = mm_nt(q, kvg_s[:, :head])
            m1 = m_s[b, rs, 0:1]
            top = jnp.maximum(m1, jnp.maximum(jnp.max(sw, axis=1, keepdims=True), jnp.max(sg, axis=1, keepdims=True)))
            pw = jnp.exp(sw - top)
            pg = jnp.exp(sg - top)
            fac = jnp.exp(m1 - top)
            tot = l_s[b, rs, 0:1] * fac + jnp.sum(pw, axis=1, keepdims=True) + jnp.sum(pg, axis=1, keepdims=True)
            o = o_s[b, rs, :] * fac + mm(pw.astype(BF16), halo_s[side, keys, head:]) + mm(pg.astype(BF16), kvg_s[:, head:])
            att_s[pl.ds(pl.multiple_of(b * BLK, BLK), BLK), h * head:(h + 1) * head] = (o / tot).astype(BF16)

    local_part(0)

    for c in swap:
        c.wait_recv()
    xh2_s[:quart, :] = (xh_s[:quart, :].astype(F32) + xa_recv[0].astype(F32)).astype(BF16)
    xh2_s[quart:, :] = (xh_s[quart:, :].astype(F32) + xa_recv[1].astype(F32)).astype(BF16)
    swap2 = [remote(xh2_s.at[pl.ds(0, quart)], xb_recv.at[0], x_ssem.at[3], x_rsem.at[3], y_peer),
             remote(xh2_s.at[pl.ds(quart, quart)], xb_recv.at[1], x_ssem.at[4], x_rsem.at[4], x_peer)]
    for c in swap2:
        c.start()

    @pl.when(has_far)
    def _():
        to_far.start()

    @pl.when(jnp.logical_not(has_far))
    def _():
        halo_s[core] = jnp.zeros(halo_s.shape[1:], BF16)

    local_part(1)
    local_part(2)

    for c in swap2:
        c.wait_recv()
    mine = core * half
    xg_all[pl.ds(mine, quart), :] = (xh2_s[:quart, :].astype(F32) + xb_recv[0].astype(F32)).astype(BF16)
    xg_all[pl.ds(mine + quart, quart), :] = (xh2_s[quart:, :].astype(F32) + xb_recv[1].astype(F32)).astype(BF16)
    spread = remote(xg_all.at[pl.ds(mine, half)], xg_all.at[pl.ds(mine, half)], x_ssem.at[5], x_rsem.at[5], partner)
    spread.start()

    local_part(3)

    remote(xg_all.at[pl.ds(half - mine, half)], xg_all.at[pl.ds(half - mine, half)], x_ssem.at[5], x_rsem.at[5], partner).wait_recv()
    xg = xg_all[...]
    kvg_s[:, :head] = mm(xg, wk_s[...]).astype(BF16)
    kvg_s[:, head:] = mm(xg, wv_s[...]).astype(BF16)
    for h in range(heads):
        qh = (mm(xg, wq_s[:, h * head:(h + 1) * head]) * head ** -0.5).astype(BF16)
        for j in range(n_dev):
            at = (j * heads + h) * per
            qg_s[at:at + per, :] = qh[j * per:(j + 1) * per]

    slab = heads * per
    for r in range(0, n_dev * slab, BLK):
        s = mm_nt(qg_s[r:r + BLK, :], kv_s[:, :head])
        top = jnp.max(s, axis=1, keepdims=True)
        p = jnp.exp(s - top)
        tot = jnp.sum(p, axis=1, keepdims=True)
        rs_send[r:r + BLK, :] = mm(p.astype(BF16), kv_s[:, head:])
        for j in range(BLK // slab):
            cut = slice(j * slab, (j + 1) * slab)
            st_send[r // slab + j, 0:1, :] = column_to_row(top[cut])
            st_send[r // slab + j, 1:2, :] = column_to_row(tot[cut])
    rs = []
    for k in range(1, n_dev):
        peer = lax.rem(me + k, n_dev)
        c = remote(rs_send.at[pl.ds(peer * slab, slab)], rs_recv.at[k], rs_ssem.at[k], rs_rsem.at[k], peer)
        c.start()
        rs.append(c)
        c = remote(st_send.at[peer], st_recv.at[k], st_ssem.at[k], st_rsem.at[k], peer)
        c.start()
        rs.append(c)

    to_near.wait_recv()
    far_part(near, width)
    far_part(near, width // 2)

    @pl.when(has_far)
    def _():
        to_far.wait_recv()

    far_part(far, width)
    far_part(far, width // 2)

    loads[4].wait()
    for b in range(n_blk):
        r = slice(b * BLK, (b + 1) * BLK)
        at = b * BLK + (per if b * BLK >= rows // 2 else 0)
        hid_ref[at:at + BLK, :] = (x_s[r, :].astype(F32) + mm(att_s[r, :], wo_s[...])).astype(BF16)

    for c in rs:
        c.wait_recv()
    rs_recv[0] = rs_send[pl.ds(me * slab, slab), :]
    st_recv[0] = st_send[me]
    top = st_recv[0, 0:1, :]
    for k in range(1, n_dev):
        top = jnp.maximum(top, st_recv[k, 0:1, :])
    tot = jnp.zeros((1, slab), F32)
    o = jnp.zeros((slab, head), F32)
    for k in range(n_dev):
        fac = jnp.exp(st_recv[k, 0:1, :] - top)
        tot = tot + st_recv[k, 1:2, :] * fac
        o = o + rs_recv[k] * row_to_column(fac)
    o = (o / row_to_column(tot)).astype(BF16)
    hg = xg_all[pl.ds(me * per, per), :].astype(F32)
    for h in range(heads):
        hg = hg + mm(o[h * per:(h + 1) * per], wo_s[h * head:(h + 1) * head, :])
    hid_ref[rows // 2:rows // 2 + per, :] = hg.astype(BF16)

    for c in [pair] + swap + swap2 + [spread] + rs + [to_near]:
        c.wait_send()

    @pl.when(has_far)
    def _():
        to_far.wait_send()


def front(x, wq, wk, wv, wo, rel_bias, gp, n_dev, heads):
    rows, dim = x.shape
    head = wk.shape[1]
    width = (rel_bias.shape[1] - 1) // 2
    n_glob = gp.shape[1]
    per = n_glob // n_dev
    n_blk = rows // BLK
    slab = heads * per
    any_spec = pl.BlockSpec(memory_space=pl.ANY)
    vmem_spec = pl.BlockSpec(memory_space=pltpu.VMEM)
    dma = pltpu.SemaphoreType.DMA
    return pl.pallas_call(
        functools.partial(front_kernel, n_dev, heads, width),
        name='front',
        out_shape=jax.ShapeDtypeStruct((rows + per, dim), BF16),
        in_specs=[any_spec] * 5 + [vmem_spec] * 2,
        out_specs=vmem_spec,
        scratch_shapes=[
            pltpu.VMEM(x.shape, BF16), pltpu.VMEM(wq.shape, BF16), pltpu.VMEM(wk.shape, BF16),
            pltpu.VMEM(wv.shape, BF16), pltpu.VMEM(wo.shape, BF16),
            pltpu.VMEM((n_blk, heads * BLK, head), BF16),
            pltpu.VMEM((rows, 2 * head), BF16), pltpu.VMEM((2, width, 2 * head), BF16),
            pltpu.VMEM((heads * BLK, BLK + 2 * width), F32), pltpu.VMEM((8, BLK + 2 * width), F32),
            pltpu.VMEM((8, rows + 2 * width), F32),
            pltpu.VMEM((n_glob, dim), BF16), pltpu.VMEM((n_glob // 2, dim), BF16), pltpu.VMEM((n_glob // 2, dim), BF16),
            pltpu.VMEM((2, n_glob // 4, dim), BF16), pltpu.VMEM((n_glob // 2, dim), BF16), pltpu.VMEM((2, n_glob // 4, dim), BF16),
            pltpu.VMEM((n_glob, dim), BF16),
            pltpu.VMEM((n_dev * slab, head), BF16), pltpu.VMEM((n_glob, 2 * head), BF16),
            pltpu.VMEM((n_blk, heads * BLK, head), F32), pltpu.VMEM((n_blk, heads * BLK, 128), F32),
            pltpu.VMEM((n_blk, heads * BLK, 128), F32),
            pltpu.VMEM((rows, heads * head), BF16),
            pltpu.VMEM((n_dev * slab, head), F32), pltpu.VMEM((n_dev, slab, head), F32),
            pltpu.VMEM((n_dev, 8, slab), F32), pltpu.VMEM((n_dev, 8, slab), F32),
            dma((5,)), dma((6,)), dma((6,)), dma((2,)), dma((2,)), dma((n_dev,)), dma((n_dev,)), dma((n_dev,)), dma((n_dev,)),
        ],
        compiler_params=pltpu.CompilerParams(collective_id=0, has_side_effects=True, vmem_limit_bytes=62 << 20),
    )(x, wq, wk, wv, wo, rel_bias, gp)


def gelu(x):
    scale = math.sqrt(2.0 / math.pi)
    part = 0.5 * x
    return part + part * jnp.tanh(x * (scale + (scale * 0.044715) * (x * x)))


def ffn_kernel(n_dev, hid_ref, w1_ref, w2_ref, ys_ref, yg_ref, acc_s, send_s, yg_s, ssem, rsem):
    part, step = pl.program_id(0), pl.program_id(1)
    last = step == pl.num_programs(1) - 1
    n_glob = yg_s.shape[0]
    per = n_glob // n_dev
    me = lax.axis_index('sp')
    tile = w1_ref.shape[1]
    rows = ys_ref.shape[0]

    def layer(lo, size):
        hi = lo + size

        @pl.when(step == 0)
        def _():
            acc_s[:size, :] = hid_ref[lo:hi, :].astype(F32)

        before = None
        for c in range(0, tile, BLK):
            s = mm(hid_ref[lo:hi, :], w1_ref[:, c:c + BLK])
            if before is not None:
                acc_s[:size, :] += mm(before, w2_ref[c - BLK:c, :])
            before = gelu(s).astype(BF16)
        acc_s[:size, :] += mm(before, w2_ref[tile - BLK:, :])

        @pl.when(last)
        def _():
            ys_ref[...] = acc_s[:rows, :].astype(BF16)

    def copy(k, peer, owner):
        return remote(send_s, yg_s.at[pl.ds(owner * per, per)], ssem.at[k], rsem.at[k], peer)

    @pl.when((part == 0) & (step == 0))
    def _():
        entry_barrier(me, n_dev)

    @pl.when(part == 0)
    def _():
        layer(0, rows + per)

    @pl.when((part == 0) & last)
    def _():
        send_s[...] = acc_s[rows:, :].astype(BF16)
        for k in range(1, n_dev):
            copy(k, lax.rem(me + k, n_dev), me).start()
        yg_s[pl.ds(me * per, per), :] = send_s[...]

    @pl.when(part == 1)
    def _():
        layer(rows + per, rows)

    @pl.when((part == 1) & last)
    def _():
        for k in range(1, n_dev):
            src = lax.rem(me + n_dev - k, n_dev)
            copy(k, src, src).wait_recv()
        yg_ref[...] = yg_s[...]
        for k in range(1, n_dev):
            copy(k, lax.rem(me + k, n_dev), me).wait_send()


def ffn(hid, w1, w2, n_glob, n_dev, tile):
    total, dim = hid.shape
    wide = w1.shape[1]
    per = n_glob // n_dev
    rows = (total - per) // 2
    dma = pltpu.SemaphoreType.DMA
    return pl.pallas_call(
        functools.partial(ffn_kernel, n_dev),
        name='ffn',
        grid=(2, wide // tile),
        out_shape=(jax.ShapeDtypeStruct((2 * rows, dim), BF16), jax.ShapeDtypeStruct((n_glob, dim), BF16)),
        in_specs=[pl.BlockSpec((total, dim), lambda p, i: (0, 0)), pl.BlockSpec((dim, tile), lambda p, i: (0, i)),
                  pl.BlockSpec((tile, dim), lambda p, i: (i, 0))],
        out_specs=(pl.BlockSpec((rows, dim), lambda p, i: (p, 0)), pl.BlockSpec((n_glob, dim), lambda p, i: (0, 0))),
        scratch_shapes=[pltpu.VMEM((rows + per, dim), F32), pltpu.VMEM((per, dim), BF16),
                        pltpu.VMEM((n_glob, dim), BF16), dma((n_dev,)), dma((n_dev,))],
        compiler_params=pltpu.CompilerParams(
            dimension_semantics=('arbitrary', 'arbitrary'), collective_id=1, has_side_effects=True, vmem_limit_bytes=60 << 20),
    )(hid, w1, w2)


def place_kernel(ys_ref, yg_ref, gp_ref, y_ref, yo_ref):
    step = pl.program_id(0)
    size = ys_ref.shape[0]
    first = (lax.axis_index('sp') * pl.num_programs(0) + step) * size
    hit = gp_ref[...] == first + lax.broadcasted_iota(jnp.int32, (size, gp_ref.shape[1]), 0)
    sel = hit.astype(F32)
    placed = mm(sel.astype(BF16), yg_ref[...]).astype(BF16)
    is_glob = jnp.max(sel, axis=1, keepdims=True) > 0.0
    y_ref[...] = jnp.where(is_glob, placed, ys_ref[...])

    @pl.when(step == 0)
    def _():
        yo_ref[...] = yg_ref[...]


def place(ys, yg, gp):
    rows, dim = ys.shape
    n_glob = yg.shape[0]
    return pl.pallas_call(
        place_kernel,
        name='place',
        grid=(rows // BLK,),
        out_shape=(jax.ShapeDtypeStruct(ys.shape, BF16), jax.ShapeDtypeStruct(yg.shape, BF16)),
        in_specs=[pl.BlockSpec((BLK, dim), lambda i: (i, 0)), pl.BlockSpec((n_glob, dim), lambda i: (0, 0)),
                  pl.BlockSpec((1, n_glob), lambda i: (0, 0))],
        out_specs=(pl.BlockSpec((BLK, dim), lambda i: (i, 0)), pl.BlockSpec((n_glob, dim), lambda i: (0, 0))),
        compiler_params=pltpu.CompilerParams(dimension_semantics=('arbitrary',)),
    )(ys, yg, gp)


def solution(mesh):
    n_dev = mesh.shape['sp']

    def shard_layer(hidden_in, w_query, w_key, w_value, w_out, w_up, w_down, rel_bias, glob_pos):
        rows, dim = hidden_in.shape
        heads, head = w_query.shape[1], w_query.shape[2]
        gp = glob_pos.reshape(1, -1)
        hid = front(hidden_in, w_query.reshape(dim, heads * head), w_key.reshape(dim, head), w_value.reshape(dim, head),
                    w_out.reshape(heads * head, dim), rel_bias, gp, n_dev, heads)
        ys, yg = ffn(hid, w_up, w_down, gp.shape[1], n_dev, 768)
        return place(ys, yg, gp)

    return jax.shard_map(
        shard_layer, mesh=mesh,
        in_specs=(P(('dp', 'sp'), None), P(), P(), P(), P(), P(), P(), P(), P('dp')),
        out_specs=(P(('dp', 'sp'), None), P('dp', None)),
        check_vma=False)
```

time: 126 us -> 103 us (0.82)
  Pallas kernels: 118 us -> 98.7 us
  local copies, waits for them, and re-layouts: 7.76 us -> 3.63 us
    pallas_call x1, Pallas kernels: 53 us -> 41 us  [front(): pl.pallas_call(functools.partial(front_kernel, n_dev, heads, width), name...]
    pallas_call x1 -> x2, Pallas kernels: 64.8 us -> 57.7 us  [the longest x1 52.8 us: ffn(): pl.pallas_call(functools.partial(ffn_kernel, n_dev), name='ffn', grid=(2,...]
    unnamed x5 -> x1, local copies, waits for them, and re-layouts: 7.76 us -> 3.63 us
where the time goes in v2:
time: 103 us
  Pallas kernels  98.7 us (96%)
  local copies, waits for them, and re-layouts  3.63 us (4%)
    pallas_call x1, Pallas kernels, ffn(): pl.pallas_call(functools.partial(ffn_kernel, n_dev), name='ffn', grid=(2,...  52.8 us
    pallas_call x1, Pallas kernels, front(): pl.pallas_call(functools.partial(front_kernel, n_dev, heads, width), name...  41 us
    pallas_call x1, Pallas kernels, place(): pl.pallas_call(place_kernel, name='place', grid=(rows // BLK,), out_shape...  4.92 us
    unnamed x1, local copies, waits for them, and re-layouts  3.63 us

profile of v2, /device:TPU:0, one launch (start us, length us, event | category | flops | bytes accessed | tf_op | source)
XLA Modules:
  0.0 103.0 jit_solution(3426955184668437761)
XLA Ops:
  0.6 3.6 %copy.11 = bf16[144,8,4,256]{3,1,2,0:T(8,128)(2,1)} copy(bf16[144,8,4,256]{3,2,1,0:T(4,128)(2,1)} %bitcast.7) | data formatting | bytes 4718592
  4.3 41.0 %front.1.hid_ref = bf16[1056,1152]{1,0:T(8,128)(2,1)} custom-call(bf16[1024,1152]{1,0:T(8,128)(2,1)} %x_hbm.1, bf16[1152,1024]{1,0:T(8,128)(2,1)} %bitcast.6, bf16[1152,256]{1,0:T(8,128)(2,1)} %bitcast.9, bf16[1152,256]{1,0:T(8,128)(2,1)} %bitcast.10, bf16[1024,1152]{1,0:T(8,128)(2,1)} %bitcast.8, f32[4,1025]{1,0:T(4,128)} %rb_ref.1, s32[1,256]{1,0:T(1,128)} %bitcast.11), custom_call_target="tpu_custom_call" | custom-call | tf_op jit(solution)/shard_map/front/pallas_call | solution.py:284
  45.3 52.8 %ffn.1 = (bf16[1024,1152]{1,0:T(8,128)(2,1)}, bf16[256,1152]{1,0:T(8,128)(2,1)}) custom-call(bf16[1056,1152]{1,0:T(8,128)(2,1)} %front.1.hid_ref, bf16[1152,6912]{1,0:T(8,128)(2,1)} %w1_ref.1, bf16[6912,1152]{1,0:T(8,128)(2,1)} %w2_ref.1), custom_call_target="tpu_custom_call" | custom-call | tf_op jit(solution)/shard_map/ffn/pallas_call | solution.py:384
  98.1 4.9 %place.1 = (bf16[1024,1152]{1,0:T(8,128)(2,1)}, bf16[256,1152]{1,0:T(8,128)(2,1)}) custom-call(bf16[1024,1152]{1,0:T(8,128)(2,1)} %get-tuple-element.4.ys_ref, bf16[256,1152]{1,0:T(8,128)(2,1)} %get-tuple-element.5.yg_ref, s32[1,256]{1,0:T(1,128)} %bitcast.12), custom_call_target="tpu_custom_call" | custom-call | tf_op jit(solution)/shard_map/place/pallas_call | solution.py:417

commit v3 on v0

v3 whole, which is shorter than its diff:
```python
import functools
import math

import jax
import jax.numpy as jnp
from jax import lax
from jax.experimental import pallas as pl
from jax.experimental.pallas import tpu as pltpu
from jax.sharding import PartitionSpec as P

BF16 = jnp.bfloat16
F32 = jnp.float32
NEG = -math.inf
BLK = 256
ROW = 32
TILE = 768
PARTS = 3


def mm(a, b):
    return jnp.dot(a, b, preferred_element_type=F32)


def mm_nt(a, b):
    return lax.dot_general(a, b, (((1,), (1,)), ((), ())), preferred_element_type=F32)


def remote(src, dst, send, recv, dev):
    return pltpu.make_async_remote_copy(
        src_ref=src, dst_ref=dst, send_sem=send, recv_sem=recv,
        device_id={'sp': dev}, device_id_type=pl.DeviceIdType.MESH)


def entry_barrier(me, n_dev):
    barrier = pltpu.get_barrier_semaphore()
    for k in range(1, n_dev):
        pl.semaphore_signal(barrier, inc=1, device_id={'sp': lax.rem(me + k, n_dev)}, device_id_type=pl.DeviceIdType.MESH)
    pl.semaphore_wait(barrier, n_dev - 1)


def diagonal(n):
    return lax.broadcasted_iota(jnp.int32, (n, n), 0) == lax.broadcasted_iota(jnp.int32, (n, n), 1)


def row_to_column(row):
    n = row.shape[1]
    return jnp.sum(jnp.where(diagonal(n), jnp.broadcast_to(row, (n, n)), 0.0), axis=1, keepdims=True)


def column_to_row(col):
    n = col.shape[0]
    return jnp.sum(jnp.where(diagonal(n), jnp.broadcast_to(col, (n, n)), 0.0), axis=0, keepdims=True)


def layer_kernel(n_dev, heads, width,
                 x_hbm, wq_hbm, wk_hbm, wv_hbm, wo_hbm, w1_hbm, w2_hbm, rb_ref, gp_ref, ys_hbm, yg_hbm,
                 x_s, wq3_s, wk_s, wv_s, wo_s, kv_s, halo_s, row_s, mask_s,
                 xg_send, xp_recv, xh_s, xa_recv, xh2_s, xb_recv, xg_all, rs_send, rs_recv, st_send, st_recv,
                 hid_s, yg_s, w1_s, w2_s,
                 in_sem, x_ssem, x_rsem, halo_ssem, halo_rsem, rs_ssem, rs_rsem, st_ssem, st_rsem, yg_ssem, yg_rsem,
                 w1_sem, w2_sem, out_sem):
    rows, dim = x_s.shape
    head = wk_s.shape[1]
    n_glob = gp_ref.shape[1]
    per = n_glob // n_dev
    slab = heads * per
    n_blk = rows // BLK
    stack = heads * BLK
    unit = stack // 2
    ext = BLK + 2 * width
    part = (rows + per) // PARTS
    split = part * (PARTS - 1) - per
    n_tile = w1_hbm.shape[1] // TILE
    me = lax.axis_index('sp')
    start = me * rows
    core = lax.rem(me, 2)
    chip = me // 2
    partner = me + 1 - 2 * core
    x_peer = 2 * (chip + 1 - 2 * lax.rem(chip, 2)) + core
    y_peer = 2 * lax.rem(chip + 2, 4) + core
    half = n_glob // 2
    quart = n_glob // 4

    def w_copies(t, slot):
        at = lax.rem(t, n_tile) * TILE
        return (pltpu.make_async_copy(w1_hbm.at[:, pl.ds(at, TILE)], w1_s.at[slot], w1_sem.at[slot]),
                pltpu.make_async_copy(w2_hbm.at[pl.ds(at, TILE), :], w2_s.at[slot], w2_sem.at[slot]))

    def rs_copies(k):
        peer = lax.rem(me + k, n_dev)
        return (remote(rs_send.at[pl.ds(peer * slab, slab)], rs_recv.at[k], rs_ssem.at[k], rs_rsem.at[k], peer),
                remote(st_send.at[peer], st_recv.at[k], st_ssem.at[k], st_rsem.at[k], peer))

    def front(wq_s, q_s, bias_s, s0, s1, p0, p1, o_s, m_s, l_s, mg_s, lg_s, att_s, qg_s):
        loads = [pltpu.make_async_copy(src, dst, in_sem.at[i]) for i, (src, dst) in enumerate(
            [(x_hbm, x_s), (wk_hbm, wk_s), (wv_hbm, wv_s), (wq_hbm, wq3_s), (wo_hbm, wo_s)])]
        for c in loads:
            c.start()
        for t in range(2):
            for c in w_copies(t, t):
                c.start()
        entry_barrier(me, n_dev)

        gp_col = row_to_column(gp_ref[...].astype(F32)).astype(jnp.int32)
        own = gp_col == start + lax.broadcasted_iota(jnp.int32, (n_glob, rows), 1)
        loads[0].wait()
        x = x_s[...]

        xg_send[...] = mm(own.astype(F32).astype(BF16), x).astype(BF16)
        pair = remote(xg_send.at[pl.ds((1 - core) * half, half)], xp_recv, x_ssem.at[0], x_rsem.at[0], partner)
        pair.start()

        loads[1].wait()
        loads[2].wait()
        kv_s[:, :head] = mm(x, wk_s[...]).astype(BF16)
        kv_s[:, head:] = mm(x, wv_s[...]).astype(BF16)

        near, far = 1 - core, core
        has_far = (me > 0) & (me < n_dev - 1)
        far_peer = lax.rem(me + n_dev - 1 + 2 * core, n_dev)

        def halo_copies(mine, theirs, peer, sem):
            return [remote(kv_s.at[pl.ds(mine * width + i * BLK, BLK)],
                           halo_s.at[theirs, pl.ds((i + theirs - 2 * i * theirs) * BLK, BLK)],
                           halo_ssem.at[sem + i], halo_rsem.at[sem + i], peer) for i in range(2)]

        to_near = halo_copies(near, core, partner, 0)
        to_far = halo_copies(far, 1 - core, far_peer, 2)
        for c in to_near:
            c.start()

        loads[3].wait()
        wq_s[...] = wq3_s[...].reshape(wq_s.shape)
        pair.wait_recv()
        xh_s[...] = (xg_send[pl.ds(core * half, half), :].astype(F32) + xp_recv[...].astype(F32)).astype(BF16)
        swap = [remote(xh_s.at[pl.ds(0, quart)], xa_recv.at[0], x_ssem.at[1], x_rsem.at[1], x_peer),
                remote(xh_s.at[pl.ds(quart, quart)], xa_recv.at[1], x_ssem.at[2], x_rsem.at[2], y_peer)]
        for c in swap:
            c.start()

        for h in range(heads):
            qh = (mm(x, wq_s[:, h * head:(h + 1) * head]) * head ** -0.5).astype(BF16)
            for b in range(n_blk):
                q_s[b, h * BLK:(h + 1) * BLK, :] = qh[b * BLK:(b + 1) * BLK]

        pos = start - width + lax.broadcasted_iota(jnp.int32, (1, rows + 2 * width), 1)
        hit = jnp.max((gp_col == pos).astype(F32), axis=0, keepdims=True) > 0.0
        bad = hit | (pos < 0) | (pos >= rows * n_dev)
        mask_s[...] = jnp.broadcast_to(jnp.where(bad, NEG, 0.0), mask_s.shape)

        row_s[...] = jnp.full(row_s.shape, NEG, F32)
        row_s[:heads, :2 * width] = rb_ref[:, :2 * width]
        last = jnp.broadcast_to(rb_ref[:, 2 * width:], (heads, 128))
        row_s[:heads, 2 * width:2 * width + 128] = jnp.where(lax.broadcasted_iota(jnp.int32, (heads, 128), 1) == 0, last, NEG)
        for h in range(heads):
            wide = jnp.broadcast_to(row_s[h:h + 1, :], (BLK, ext))
            bias_s[h * BLK:(h + 1) * BLK, :] = pltpu.roll(wide, 0, 1, stride=1, stride_axis=0)

        class Local:
            def __init__(self, b, g, before=None):
                self.b, self.r0, self.before = b, g * unit, before
                self.lo, self.hi = max(0, b * BLK - width), min(rows, (b + 1) * BLK + width)

            def score(self, s_ref):
                s_ref[:, :self.hi - self.lo] = mm_nt(q_s[self.b, self.r0:self.r0 + unit], kv_s[self.lo:self.hi, :head])

            def soft(self, s_ref, p_ref):
                n, c0 = self.hi - self.lo, self.lo - self.b * BLK + width
                for r in range(0, unit, ROW):
                    rs, ra = slice(r, r + ROW), slice(self.r0 + r, self.r0 + r + ROW)
                    s = s_ref[rs, :n] + bias_s[ra, c0:c0 + n] + mask_s[0:1, width + self.lo:width + self.hi]
                    top = jnp.max(s, axis=1, keepdims=True)
                    p = jnp.exp(s - top)
                    p_ref[rs, :n] = p.astype(BF16)
                    m_s[self.b, ra, :] = jnp.broadcast_to(top, (ROW, 128))
                    l_s[self.b, ra, :] = jnp.broadcast_to(jnp.sum(p, axis=1, keepdims=True), (ROW, 128))

            def value(self, p_ref):
                o_s[self.b, self.r0:self.r0 + unit] = mm(p_ref[:, :self.hi - self.lo], kv_s[self.lo:self.hi, head:])

        class Global:
            def __init__(self, g, before=None):
                self.r0, self.before = g * unit, before

            def score(self, s_ref):
                s_ref[...] = mm_nt(qg_s[self.r0:self.r0 + unit, :], kv_s[:, :head])

            def soft(self, s_ref, p_ref):
                for r in range(0, unit, ROW):
                    rs = slice(r, r + ROW)
                    s = s_ref[rs, :]
                    top = jnp.max(s, axis=1, keepdims=True)
                    p = jnp.exp(s - top)
                    p_ref[rs, :] = p.astype(BF16)
                    mg_s[rs, :] = jnp.broadcast_to(top, (ROW, 128))
                    lg_s[rs, :] = jnp.broadcast_to(jnp.sum(p, axis=1, keepdims=True), (ROW, 128))
                for j in range(unit // slab):
                    cut, to = slice(j * slab, (j + 1) * slab), self.r0 // slab + j
                    st_send[to, 0:1, :] = jnp.sum(jnp.where(diagonal(slab), mg_s[cut, :], 0.0), axis=0, keepdims=True)
                    st_send[to, 1:2, :] = jnp.sum(jnp.where(diagonal(slab), lg_s[cut, :], 0.0), axis=0, keepdims=True)

            def value(self, p_ref):
                rs_send[self.r0:self.r0 + unit, :] = mm(p_ref[...], kv_s[:, head:])

        class Far:
            def __init__(self, side, inner, g, before=None):
                self.side, self.inner, self.r0, self.before = side, inner, g * unit, before
                self.b = 1 + side * (n_blk - 3) if inner else side * (n_blk - 1)
                self.k0, self.n = (BLK, 2 * BLK) if inner else (0, 3 * BLK)

            def score(self, s_ref):
                s_ref[:, :self.n] = mm_nt(q_s[self.b, self.r0:self.r0 + unit], halo_s[self.side, self.k0:, :head])

            def soft(self, s_ref, p_ref):
                side, n = self.side, self.n
                near_mask = BLK + side * (rows + BLK)
                if self.inner:
                    cuts = [(side * (ext - BLK), near_mask)]
                else:
                    cuts = [(side * (ext - BLK), side * (rows + width + BLK)), (BLK + side * (ext - 3 * BLK), near_mask)]
                for r in range(0, unit, ROW):
                    rs, ra = slice(r, r + ROW), slice(self.r0 + r, self.r0 + r + ROW)
                    pieces = []
                    for i, (c0, m0) in enumerate(cuts):
                        pieces.append(s_ref[rs, i * BLK:(i + 1) * BLK] + bias_s[ra, pl.ds(pl.multiple_of(c0, BLK), BLK)]
                                      + mask_s[0:1, pl.ds(pl.multiple_of(m0, BLK), BLK)])
                    pieces.append(s_ref[rs, n - BLK:n])
                    s = jnp.concatenate(pieces, axis=1)
                    m1 = m_s[self.b, ra, :]
                    top = jnp.maximum(m1, jnp.broadcast_to(jnp.max(s, axis=1, keepdims=True), (ROW, 128)))
                    p = jnp.exp(s - jnp.concatenate([top] * (n // 128), axis=1))
                    p_ref[rs, :n] = p.astype(BF16)
                    fac = jnp.exp(m1 - top)
                    inv = 1.0 / (l_s[self.b, ra, :] * fac + jnp.broadcast_to(jnp.sum(p, axis=1, keepdims=True), (ROW, 128)))
                    m_s[self.b, ra, :] = fac * inv
                    l_s[self.b, ra, :] = inv

            def value(self, p_ref):
                at = pl.ds(pl.multiple_of(self.b * BLK, BLK), BLK)
                new = mm(p_ref[:, :self.n], halo_s[self.side, self.k0:, head:])
                for h in range(unit // BLK):
                    ra = slice(self.r0 + h * BLK, self.r0 + (h + 1) * BLK)
                    fac, inv = m_s[self.b, ra, :], l_s[self.b, ra, :]
                    o = (o_s[self.b, ra, :] * jnp.concatenate([fac] * (head // 128), axis=1)
                         + new[h * BLK:(h + 1) * BLK] * jnp.concatenate([inv] * (head // 128), axis=1))
                    col = (self.r0 // BLK + h) * head
                    att_s[at, col:col + head] = o.astype(BF16)

        swap2 = [remote(xh2_s.at[pl.ds(0, quart)], xb_recv.at[0], x_ssem.at[3], x_rsem.at[3], y_peer),
                 remote(xh2_s.at[pl.ds(quart, quart)], xb_recv.at[1], x_ssem.at[4], x_rsem.at[4], x_peer)]
        mine = core * half
        spread = remote(xg_all.at[pl.ds(mine, half)], xg_all.at[pl.ds(mine, half)], x_ssem.at[5], x_rsem.at[5], partner)

        def second_swap():
            for c in swap:
                c.wait_recv()
            xh2_s[:quart, :] = (xh_s[:quart, :].astype(F32) + xa_recv[0].astype(F32)).astype(BF16)
            xh2_s[quart:, :] = (xh_s[quart:, :].astype(F32) + xa_recv[1].astype(F32)).astype(BF16)
            for c in swap2:
                c.start()

            @pl.when(has_far)
            def _():
                for c in to_far:
                    c.start()

            @pl.when(jnp.logical_not(has_far))
            def _():
                halo_s[core, :2 * BLK, :] = jnp.zeros((2 * BLK, 2 * head), BF16)

        def share():
            for c in swap2:
                c.wait_recv()
            xg_all[pl.ds(mine, quart), :] = (xh2_s[:quart, :].astype(F32) + xb_recv[0].astype(F32)).astype(BF16)
            xg_all[pl.ds(mine + quart, quart), :] = (xh2_s[quart:, :].astype(F32) + xb_recv[1].astype(F32)).astype(BF16)
            spread.start()

        def project_global():
            theirs = xg_all.at[pl.ds(half - mine, half)]
            remote(theirs, theirs, x_ssem.at[5], x_rsem.at[5], partner).wait_recv()
            xg = xg_all[...]
            for h in range(heads):
                qh = (mm(xg, wq_s[:, h * head:(h + 1) * head]) * head ** -0.5).astype(BF16)
                for j in range(n_dev):
                    at = (j * heads + h) * per
                    qg_s[at:at + per, :] = qh[j * per:(j + 1) * per]
            for j, w in enumerate((wk_s, wv_s)):
                both = mm(xg, w[...]).astype(BF16)
                for side in range(2):
                    halo_s[side, 2 * BLK:, j * head:(j + 1) * head] = both

        def near_ready():
            for c in to_near:
                c.wait_recv()

        def start_partials():
            for k in range(1, n_dev):
                for c in rs_copies(k):
                    c.start()

        def wait_far():
            @pl.when(has_far)
            def _():
                for c in to_far:
                    c.wait_recv()

        hooks = {2: second_swap, 7: share}
        units = [Local(i // 2, i % 2, hooks.get(i)) for i in range(2 * n_blk)]
        units += [Global(0, project_global), Global(1)]
        units += [Far(near, False, 0, near_ready), Far(near, False, 1, start_partials), Far(near, True, 0), Far(near, True, 1)]
        units += [Far(far, False, 0, wait_far), Far(far, False, 1), Far(far, True, 0), Far(far, True, 1)]
        s_refs, p_refs = (s0, s1), (p0, p1)
        for i, u in enumerate(units):
            for k in ((0, 1) if i == 0 else (i + 1,)):
                if k < len(units):
                    if units[k].before is not None:
                        units[k].before()
                    units[k].score(s_refs[k % 2])
            u.soft(s_refs[i % 2], p_refs[i % 2])
            u.value(p_refs[i % 2])

        loads[4].wait()
        for b in range(n_blk):
            r0, r1 = b * BLK, (b + 1) * BLK
            res = (x_s[r0:r1, :].astype(F32) + mm(att_s[r0:r1, :], wo_s[...])).astype(BF16)
            cut = min(max(split - r0, 0), BLK)
            if cut:
                hid_s[r0:r0 + cut, :] = res[:cut]
            if cut < BLK:
                hid_s[r0 + cut + per:r1 + per, :] = res[cut:]

        for c in [pair] + swap + swap2 + [spread] + to_near:
            c.wait_send()

        @pl.when(has_far)
        def _():
            for c in to_far:
                c.wait_send()

    def finish_global():
        for k in range(1, n_dev):
            for c in rs_copies(k):
                c.wait()
        rs_recv[0] = rs_send[pl.ds(me * slab, slab), :]
        st_recv[0] = st_send[me]
        top = st_recv[0, 0:1, :]
        for k in range(1, n_dev):
            top = jnp.maximum(top, st_recv[k, 0:1, :])
        tot = jnp.zeros((1, slab), F32)
        o = jnp.zeros((slab, head), F32)
        for k in range(n_dev):
            fac = jnp.exp(st_recv[k, 0:1, :] - top)
            tot = tot + st_recv[k, 1:2, :] * fac
            o = o + rs_recv[k] * row_to_column(fac)
        o = (o / row_to_column(tot)).astype(BF16)
        hg = xg_all[pl.ds(me * per, per), :].astype(F32)
        for h in range(heads):
            hg = hg + mm(o[h * per:(h + 1) * per], wo_s[h * head:(h + 1) * head, :])
        hid_s[split:split + per, :] = hg.astype(BF16)

    def yg_copy(k, peer, owner):
        return remote(hid_s.at[pl.ds(split, per)], yg_s.at[pl.ds(owner * per, per)], yg_ssem.at[k], yg_rsem.at[k], peer)

    def out_copy(p):
        lo, hi = p * part, min((p + 1) * part, split) if p < PARTS - 1 else rows
        if p == PARTS - 1:
            lo = split
        shift = per if p == PARTS - 1 else 0
        return pltpu.make_async_copy(hid_s.at[pl.ds(lo + shift, hi - lo)], ys_hbm.at[pl.ds(lo, hi - lo)], out_sem.at[p])

    def feed_forward(acc_s, u_s):
        for p in range(PARTS):
            r0, r1 = p * part, (p + 1) * part
            if p == PARTS - 2:
                finish_global()
            acc_s[...] = hid_s[r0:r1, :].astype(F32)
            u_s[...] = jnp.zeros_like(u_s)

            def step(i, carry):
                t = p * n_tile + i
                slot, prev = lax.rem(t, 3), lax.rem(t + 2, 3)
                for c in w_copies(t, slot):
                    c.wait()
                s = mm(hid_s[r0:r1, :], w1_s[slot, :, :BLK])
                acc_s[...] += mm(u_s[...], w2_s[prev, TILE - BLK:, :])
                u = gelu(s).astype(BF16)
                for c in range(BLK, TILE, BLK):
                    s = mm(hid_s[r0:r1, :], w1_s[slot, :, c:c + BLK])
                    acc_s[...] += mm(u, w2_s[slot, c - BLK:c, :])
                    u = gelu(s).astype(BF16)
                u_s[...] = u

                @pl.when(t + 2 < PARTS * n_tile)
                def _():
                    for c in w_copies(t + 2, prev):
                        c.start()

                return carry

            lax.fori_loop(0, n_tile, step, 0)
            slot = ((p + 1) * n_tile - 1) % 3
            hid_s[r0:r1, :] = (acc_s[...] + mm(u_s[...], w2_s[slot, TILE - BLK:, :])).astype(BF16)
            out_copy(p).start()
            if p == PARTS - 2:
                for k in range(1, n_dev):
                    yg_copy(k, lax.rem(me + k, n_dev), me).start()
                yg_s[pl.ds(me * per, per), :] = hid_s[split:split + per, :]

    w2_s[2, TILE - BLK:, :] = jnp.zeros((BLK, dim), BF16)
    pl.run_scoped(
        front,
        pltpu.VMEM((dim, heads * head), BF16), pltpu.VMEM((n_blk, stack, head), BF16), pltpu.VMEM((stack, ext), F32),
        pltpu.VMEM((unit, rows), F32), pltpu.VMEM((unit, rows), F32), pltpu.VMEM((unit, rows), BF16), pltpu.VMEM((unit, rows), BF16),
        pltpu.VMEM((n_blk, stack, head), F32), pltpu.VMEM((n_blk, stack, 128), F32), pltpu.VMEM((n_blk, stack, 128), F32),
        pltpu.VMEM((unit, 128), F32), pltpu.VMEM((unit, 128), F32),
        pltpu.VMEM((rows, heads * head), BF16), pltpu.VMEM((n_dev * slab, head), BF16))
    pl.run_scoped(feed_forward, pltpu.VMEM((part, dim), F32), pltpu.VMEM((part, BLK), BF16))
    for k in range(1, n_dev):
        src = lax.rem(me + n_dev - k, n_dev)
        yg_copy(k, src, src).wait_recv()
    last = pltpu.make_async_copy(yg_s, yg_hbm, out_sem.at[PARTS])
    last.start()
    for k in range(1, n_dev):
        yg_copy(k, lax.rem(me + k, n_dev), me).wait_send()
    for p in range(PARTS):
        out_copy(p).wait()
    last.wait()


def gelu(x):
    scale = math.sqrt(2.0 / math.pi)
    part = 0.5 * x
    return part + part * jnp.tanh(x * (scale + (scale * 0.044715) * (x * x)))


def layer(x, wq, wk, wv, wo, w1, w2, rel_bias, gp, n_dev):
    rows, dim = x.shape
    heads, head = wq.shape[1:]
    width = (rel_bias.shape[1] - 1) // 2
    n_glob = gp.shape[1]
    per = n_glob // n_dev
    slab = heads * per
    any_spec = pl.BlockSpec(memory_space=pl.ANY)
    vmem_spec = pl.BlockSpec(memory_space=pltpu.VMEM)
    dma = pltpu.SemaphoreType.DMA
    return pl.pallas_call(
        functools.partial(layer_kernel, n_dev, heads, width),
        name='layer',
        out_shape=(jax.ShapeDtypeStruct((rows, dim), BF16), jax.ShapeDtypeStruct((n_glob, dim), BF16)),
        in_specs=[any_spec] * 7 + [vmem_spec] * 2,
        out_specs=(any_spec, any_spec),
        scratch_shapes=[
            pltpu.VMEM(x.shape, BF16), pltpu.VMEM(wq.shape, BF16), pltpu.VMEM(wk.shape, BF16),
            pltpu.VMEM(wv.shape, BF16), pltpu.VMEM(wo.shape, BF16),
            pltpu.VMEM((rows, 2 * head), BF16), pltpu.VMEM((2, 3 * BLK, 2 * head), BF16),
            pltpu.VMEM((8, BLK + 2 * width), F32), pltpu.VMEM((8, rows + 2 * width), F32),
            pltpu.VMEM((n_glob, dim), BF16), pltpu.VMEM((n_glob // 2, dim), BF16), pltpu.VMEM((n_glob // 2, dim), BF16),
            pltpu.VMEM((2, n_glob // 4, dim), BF16), pltpu.VMEM((n_glob // 2, dim), BF16), pltpu.VMEM((2, n_glob // 4, dim), BF16),
            pltpu.VMEM((n_glob, dim), BF16),
            pltpu.VMEM((n_dev * slab, head), F32), pltpu.VMEM((n_dev, slab, head), F32),
            pltpu.VMEM((n_dev, 8, slab), F32), pltpu.VMEM((n_dev, 8, slab), F32),
            pltpu.VMEM((rows + per, dim), BF16), pltpu.VMEM((n_glob, dim), BF16),
            pltpu.VMEM((3, dim, TILE), BF16), pltpu.VMEM((3, TILE, dim), BF16),
            dma((5,)), dma((6,)), dma((6,)), dma((4,)), dma((4,)), dma((n_dev,)), dma((n_dev,)), dma((n_dev,)), dma((n_dev,)),
            dma((n_dev,)), dma((n_dev,)), dma((3,)), dma((3,)), dma((PARTS + 1,)),
        ],
        compiler_params=pltpu.CompilerParams(collective_id=0, has_side_effects=True, vmem_limit_bytes=67043328),
    )(x, wq, wk, wv, wo, w1, w2, rel_bias, gp)


def place_kernel(ys_hbm, yg_hbm, gp_ref, y_hbm, yo_hbm, ys_s, y_s, yg_s, in_sem, out_sem):
    n = ys_s.shape[0]
    n_glob = gp_ref.shape[1]
    gets = [pltpu.make_async_copy(ys_hbm.at[pl.ds(i * BLK, BLK)], ys_s.at[i], in_sem.at[i]) for i in range(n)]
    puts = [pltpu.make_async_copy(y_s.at[i], y_hbm.at[pl.ds(i * BLK, BLK)], out_sem.at[i]) for i in range(n)]
    get_g = pltpu.make_async_copy(yg_hbm, yg_s, in_sem.at[n])
    put_g = pltpu.make_async_copy(yg_s, yo_hbm, out_sem.at[n])
    get_g.start()
    for c in gets:
        c.start()
    get_g.wait()
    put_g.start()
    for i in range(n):
        first = (lax.axis_index('sp') * n + i) * BLK
        hit = gp_ref[...] == first + lax.broadcasted_iota(jnp.int32, (BLK, n_glob), 0)
        sel = hit.astype(F32)
        placed = mm(sel.astype(BF16), yg_s[...]).astype(BF16)
        is_glob = jnp.max(sel, axis=1, keepdims=True) > 0.0
        gets[i].wait()
        y_s[i] = jnp.where(is_glob, placed, ys_s[i])
        puts[i].start()
    for c in puts:
        c.wait()
    put_g.wait()


def place(ys, yg, gp):
    rows, dim = ys.shape
    n = rows // BLK
    any_spec = pl.BlockSpec(memory_space=pl.ANY)
    dma = pltpu.SemaphoreType.DMA
    return pl.pallas_call(
        place_kernel,
        name='place',
        out_shape=(jax.ShapeDtypeStruct(ys.shape, BF16), jax.ShapeDtypeStruct(yg.shape, BF16)),
        in_specs=[any_spec, any_spec, pl.BlockSpec(memory_space=pltpu.VMEM)],
        out_specs=(any_spec, any_spec),
        scratch_shapes=[pltpu.VMEM((n, BLK, dim), BF16), pltpu.VMEM((n, BLK, dim), BF16), pltpu.VMEM(yg.shape, BF16),
                        dma((n + 1,)), dma((n + 1,))],
        compiler_params=pltpu.CompilerParams(vmem_limit_bytes=60 << 20),
    )(ys, yg, gp)


def solution(mesh):
    n_dev = mesh.shape['sp']

    def shard_layer(hidden_in, w_query, w_key, w_value, w_out, w_up, w_down, rel_bias, glob_pos):
        dim = hidden_in.shape[1]
        heads, head = w_query.shape[1], w_query.shape[2]
        gp = glob_pos.reshape(1, -1)
        ys, yg = layer(hidden_in, w_query, w_key.reshape(dim, head), w_value.reshape(dim, head),
                       w_out.reshape(heads * head, dim), w_up, w_down, rel_bias, gp, n_dev)
        return place(ys, yg, gp)

    return jax.shard_map(
        shard_layer, mesh=mesh,
        in_specs=(P(('dp', 'sp'), None), P(), P(), P(), P(), P(), P(), P(), P('dp')),
        out_specs=(P(('dp', 'sp'), None), P('dp', None)),
        check_vma=False)
```

time: 352 us -> 91.6 us (0.26)
  the two profiles are of different devices: /device:TPU:0 before, /device:TPU:1 now
where the time goes in v3:
time: 91.6 us; the launch traced here: 91.4 us
  Pallas kernels  90.6 us (99%)
    pallas_call x1, Pallas kernels, layer(): pl.pallas_call(functools.partial(layer_kernel, n_dev, heads, width), name...  86.1 us
    pallas_call x1, Pallas kernels, place(): pl.pallas_call(place_kernel, name='place', out_shape=(jax.ShapeDtypeStruc...  4.5 us

profile of v3, /device:TPU:1, one launch (start us, length us, event | category | flops | bytes accessed | tf_op | source)
XLA Modules:
  0.0 91.4 jit_solution(10347790147579000370)
XLA Ops:
  0.6 86.1 %layer.1 = (bf16[1024,1152]{1,0:T(8,128)(2,1)}, bf16[256,1152]{1,0:T(8,128)(2,1)}) custom-call(bf16[1024,1152]{1,0:T(8,128)(2,1)} %x_hbm.1, bf16[1152,4,256]{2,1,0:T(4,128)(2,1)} %wq_hbm.1, bf16[1152,256]{1,0:T(8,128)(2,1)} %bitcast.5, bf16[1152,256]{1,0:T(8,128)(2,1)} %bitcast.6, bf16[1024,1152]{1,0:T(8,128)(2,1)} %bitcast.4, bf16[1152,6912]{1,0:T(8,128)(2,1)} %w1_hbm.1, ...), custom_call_target="tpu_custom_call" | custom-call | tf_op jit(solution)/shard_map/layer/pallas_call | solution.py:446
  86.7 4.5 %place.1 = (bf16[1024,1152]{1,0:T(8,128)(2,1)}, bf16[256,1152]{1,0:T(8,128)(2,1)}) custom-call(bf16[1024,1152]{1,0:T(8,128)(2,1)} %get-tuple-element.4.ys_hbm, bf16[256,1152]{1,0:T(8,128)(2,1)} %get-tuple-element.5.yg_hbm, s32[1,256]{1,0:T(1,128)} %bitcast.8), custom_call_target="tpu_custom_call" | custom-call | tf_op jit(solution)/shard_map/place/pallas_call | solution.py:502

commit v4 on v3

--- a/solution.py
+++ b/solution.py
@@ -13,8 +13,11 @@
 NEG = -math.inf
 BLK = 256
 ROW = 32
-TILE = 768
+PIECE = 128
 PARTS = 3
+UNROLL = 9
+W1_CUT = ((0, 5), (5, 4))
+W2_CUT = ((0, 4), (4, 4), (8, 1))
 
 
 def mm(a, b):
@@ -50,6 +53,13 @@
 def column_to_row(col):
     n = col.shape[0]
     return jnp.sum(jnp.where(diagonal(n), jnp.broadcast_to(col, (n, n)), 0.0), axis=0, keepdims=True)
+
+
+def lane_max(s):
+    best = s[:, :128]
+    for c in range(128, s.shape[1], 128):
+        best = jnp.maximum(best, s[:, c:c + 128])
+    return best
 
 
 def layer_kernel(n_dev, heads, width,
@@ -70,7 +80,7 @@
     ext = BLK + 2 * width
     part = (rows + per) // PARTS
     split = part * (PARTS - 1) - per
-    n_tile = w1_hbm.shape[1] // TILE
+    n_chunk = w1_hbm.shape[1] // BLK
     me = lax.axis_index('sp')
     start = me * rows
     core = lax.rem(me, 2)
@@ -81,29 +91,50 @@
     half = n_glob // 2
     quart = n_glob // 4
 
-    def w_copies(t, slot):
-        at = lax.rem(t, n_tile) * TILE
-        return (pltpu.make_async_copy(w1_hbm.at[:, pl.ds(at, TILE)], w1_s.at[slot], w1_sem.at[slot]),
-                pltpu.make_async_copy(w2_hbm.at[pl.ds(at, TILE), :], w2_s.at[slot], w2_sem.at[slot]))
+    n_part = n_chunk // UNROLL
+
+    def w1_copy(i, turn):
+        lo, n = W1_CUT[i]
+        at = lax.rem(turn, n_part) * (UNROLL * BLK) + lo * BLK
+        return pltpu.make_async_copy(w1_hbm.at[:, pl.ds(at, n * BLK)], w1_s.at[:, pl.ds(lo * BLK, n * BLK)], w1_sem.at[i])
+
+    def w2_copy(i, turn):
+        lo, n = W2_CUT[i]
+        at = lax.rem(turn, n_part) * (UNROLL * BLK) + lo * BLK
+        return pltpu.make_async_copy(w2_hbm.at[pl.ds(at, n * BLK), :], w2_s.at[pl.ds(lo * BLK, n * BLK), :], w2_sem.at[i])
+
+    def first_weights():
+        return [w1_copy(0, 0), w2_copy(2, 0), w2_copy(0, 0), w1_copy(1, 0), w2_copy(1, 0)]
 
     def rs_copies(k):
         peer = lax.rem(me + k, n_dev)
         return (remote(rs_send.at[pl.ds(peer * slab, slab)], rs_recv.at[k], rs_ssem.at[k], rs_rsem.at[k], peer),
                 remote(st_send.at[peer], st_recv.at[k], st_ssem.at[k], st_rsem.at[k], peer))
 
-    def front(wq_s, q_s, bias_s, s0, s1, p0, p1, o_s, m_s, l_s, mg_s, lg_s, att_s, qg_s):
+    def front(wq_s, q_s, bias_s, s0, s1, t0, t1, p0, p1, o_s, m_s, l_s, mg_s, lg_s, att_s, qg_s):
         loads = [pltpu.make_async_copy(src, dst, in_sem.at[i]) for i, (src, dst) in enumerate(
             [(x_hbm, x_s), (wk_hbm, wk_s), (wv_hbm, wv_s), (wq_hbm, wq3_s), (wo_hbm, wo_s)])]
-        for c in loads:
+        for c in loads[:3]:
             c.start()
-        for t in range(2):
-            for c in w_copies(t, t):
-                c.start()
         entry_barrier(me, n_dev)
 
         gp_col = row_to_column(gp_ref[...].astype(F32)).astype(jnp.int32)
         own = gp_col == start + lax.broadcasted_iota(jnp.int32, (n_glob, rows), 1)
+        pos = start - width + lax.broadcasted_iota(jnp.int32, (1, rows + 2 * width), 1)
+        hit = jnp.max((gp_col == pos).astype(F32), axis=0, keepdims=True) > 0.0
+        bad = hit | (pos < 0) | (pos >= rows * n_dev)
+        mask_s[...] = jnp.broadcast_to(jnp.where(bad, NEG, 0.0), mask_s.shape)
+
+        row_s[...] = jnp.full(row_s.shape, NEG, F32)
+        row_s[:heads, :2 * width] = rb_ref[:, :2 * width]
+        last = jnp.broadcast_to(rb_ref[:, 2 * width:], (heads, 128))
+        row_s[:heads, 2 * width:2 * width + 128] = jnp.where(lax.broadcasted_iota(jnp.int32, (heads, 128), 1) == 0, last, NEG)
+        for h in range(heads):
+            wide = jnp.broadcast_to(row_s[h:h + 1, :], (BLK, ext))
+            bias_s[h * BLK:(h + 1) * BLK, :] = pltpu.roll(wide, 0, 1, stride=1, stride_axis=0)
+
         loads[0].wait()
+        loads[3].start()
         x = x_s[...]
 
         xg_send[...] = mm(own.astype(F32).astype(BF16), x).astype(BF16)
@@ -124,6 +155,9 @@
                            halo_s.at[theirs, pl.ds((i + theirs - 2 * i * theirs) * BLK, BLK)],
                            halo_ssem.at[sem + i], halo_rsem.at[sem + i], peer) for i in range(2)]
 
+        loads[4].start()
+        for c in first_weights():
+            c.start()
         to_near = halo_copies(near, core, partner, 0)
         to_far = halo_copies(far, 1 - core, far_peer, 2)
         for c in to_near:
@@ -143,34 +177,24 @@
             for b in range(n_blk):
                 q_s[b, h * BLK:(h + 1) * BLK, :] = qh[b * BLK:(b + 1) * BLK]
 
-        pos = start - width + lax.broadcasted_iota(jnp.int32, (1, rows + 2 * width), 1)
-        hit = jnp.max((gp_col == pos).astype(F32), axis=0, keepdims=True) > 0.0
-        bad = hit | (pos < 0) | (pos >= rows * n_dev)
-        mask_s[...] = jnp.broadcast_to(jnp.where(bad, NEG, 0.0), mask_s.shape)
-
-        row_s[...] = jnp.full(row_s.shape, NEG, F32)
-        row_s[:heads, :2 * width] = rb_ref[:, :2 * width]
-        last = jnp.broadcast_to(rb_ref[:, 2 * width:], (heads, 128))
-        row_s[:heads, 2 * width:2 * width + 128] = jnp.where(lax.broadcasted_iota(jnp.int32, (heads, 128), 1) == 0, last, NEG)
-        for h in range(heads):
-            wide = jnp.broadcast_to(row_s[h:h + 1, :], (BLK, ext))
-            bias_s[h * BLK:(h + 1) * BLK, :] = pltpu.roll(wide, 0, 1, stride=1, stride_axis=0)
-
         class Local:
             def __init__(self, b, g, before=None):
                 self.b, self.r0, self.before = b, g * unit, before
                 self.lo, self.hi = max(0, b * BLK - width), min(rows, (b + 1) * BLK + width)
 
-            def score(self, s_ref):
-                s_ref[:, :self.hi - self.lo] = mm_nt(q_s[self.b, self.r0:self.r0 + unit], kv_s[self.lo:self.hi, :head])
-
-            def soft(self, s_ref, p_ref):
+            def score(self, s_ref, t_ref):
                 n, c0 = self.hi - self.lo, self.lo - self.b * BLK + width
+                s = mm_nt(q_s[self.b, self.r0:self.r0 + unit], kv_s[self.lo:self.hi, :head])
+                s = s + bias_s[self.r0:self.r0 + unit, c0:c0 + n] + mask_s[0:1, width + self.lo:width + self.hi]
+                s_ref[:, :n] = s
+                t_ref[...] = lane_max(s)
+
+            def soft(self, s_ref, t_ref, p_ref):
+                n = self.hi - self.lo
                 for r in range(0, unit, ROW):
                     rs, ra = slice(r, r + ROW), slice(self.r0 + r, self.r0 + r + ROW)
-                    s = s_ref[rs, :n] + bias_s[ra, c0:c0 + n] + mask_s[0:1, width + self.lo:width + self.hi]
-                    top = jnp.max(s, axis=1, keepdims=True)
-                    p = jnp.exp(s - top)
+                    top = jnp.max(t_ref[rs, :], axis=1, keepdims=True)
+                    p = jnp.exp(s_ref[rs, :n] - top)
                     p_ref[rs, :n] = p.astype(BF16)
                     m_s[self.b, ra, :] = jnp.broadcast_to(top, (ROW, 128))
                     l_s[self.b, ra, :] = jnp.broadcast_to(jnp.sum(p, axis=1, keepdims=True), (ROW, 128))
@@ -182,15 +206,16 @@
             def __init__(self, g, before=None):
                 self.r0, self.before = g * unit, before
 
-            def score(self, s_ref):
-                s_ref[...] = mm_nt(qg_s[self.r0:self.r0 + unit, :], kv_s[:, :head])
-
-            def soft(self, s_ref, p_ref):
+            def score(self, s_ref, t_ref):
+                s = mm_nt(qg_s[self.r0:self.r0 + unit, :], kv_s[:, :head])
+                s_ref[...] = s
+                t_ref[...] = lane_max(s)
+
+            def soft(self, s_ref, t_ref, p_ref):
                 for r in range(0, unit, ROW):
                     rs = slice(r, r + ROW)
-                    s = s_ref[rs, :]
-                    top = jnp.max(s, axis=1, keepdims=True)
-                    p = jnp.exp(s - top)
+                    top = jnp.max(t_ref[rs, :], axis=1, keepdims=True)
+                    p = jnp.exp(s_ref[rs, :] - top)
                     p_ref[rs, :] = p.astype(BF16)
                     mg_s[rs, :] = jnp.broadcast_to(top, (ROW, 128))
                     lg_s[rs, :] = jnp.broadcast_to(jnp.sum(p, axis=1, keepdims=True), (ROW, 128))
@@ -208,26 +233,30 @@
                 self.b = 1 + side * (n_blk - 3) if inner else side * (n_blk - 1)
                 self.k0, self.n = (BLK, 2 * BLK) if inner else (0, 3 * BLK)
 
-            def score(self, s_ref):
-                s_ref[:, :self.n] = mm_nt(q_s[self.b, self.r0:self.r0 + unit], halo_s[self.side, self.k0:, :head])
-
-            def soft(self, s_ref, p_ref):
+            def score(self, s_ref, t_ref):
                 side, n = self.side, self.n
                 near_mask = BLK + side * (rows + BLK)
                 if self.inner:
                     cuts = [(side * (ext - BLK), near_mask)]
                 else:
                     cuts = [(side * (ext - BLK), side * (rows + width + BLK)), (BLK + side * (ext - 3 * BLK), near_mask)]
+                s = mm_nt(q_s[self.b, self.r0:self.r0 + unit], halo_s[side, self.k0:, :head])
+                best = lane_max(s[:, n - BLK:])
+                s_ref[:, n - BLK:n] = s[:, n - BLK:]
+                for i, (c0, m0) in enumerate(cuts):
+                    cut = (s[:, i * BLK:(i + 1) * BLK] + bias_s[self.r0:self.r0 + unit, pl.ds(pl.multiple_of(c0, BLK), BLK)]
+                           + mask_s[0:1, pl.ds(pl.multiple_of(m0, BLK), BLK)])
+                    s_ref[:, i * BLK:(i + 1) * BLK] = cut
+                    best = jnp.maximum(best, lane_max(cut))
+                t_ref[...] = best
+
+            def soft(self, s_ref, t_ref, p_ref):
+                n = self.n
                 for r in range(0, unit, ROW):
                     rs, ra = slice(r, r + ROW), slice(self.r0 + r, self.r0 + r + ROW)
-                    pieces = []
-                    for i, (c0, m0) in enumerate(cuts):
-                        pieces.append(s_ref[rs, i * BLK:(i + 1) * BLK] + bias_s[ra, pl.ds(pl.multiple_of(c0, BLK), BLK)]
-                                      + mask_s[0:1, pl.ds(pl.multiple_of(m0, BLK), BLK)])
-                    pieces.append(s_ref[rs, n - BLK:n])
-                    s = jnp.concatenate(pieces, axis=1)
                     m1 = m_s[self.b, ra, :]
-                    top = jnp.maximum(m1, jnp.broadcast_to(jnp.max(s, axis=1, keepdims=True), (ROW, 128)))
+                    top = jnp.maximum(m1, jnp.broadcast_to(jnp.max(t_ref[rs, :], axis=1, keepdims=True), (ROW, 128)))
+                    s = s_ref[rs, :n]
                     p = jnp.exp(s - jnp.concatenate([top] * (n // 128), axis=1))
                     p_ref[rs, :n] = p.astype(BF16)
                     fac = jnp.exp(m1 - top)
@@ -309,14 +338,14 @@
         units += [Global(0, project_global), Global(1)]
         units += [Far(near, False, 0, near_ready), Far(near, False, 1, start_partials), Far(near, True, 0), Far(near, True, 1)]
         units += [Far(far, False, 0, wait_far), Far(far, False, 1), Far(far, True, 0), Far(far, True, 1)]
-        s_refs, p_refs = (s0, s1), (p0, p1)
+        s_refs, t_refs, p_refs = (s0, s1), (t0, t1), (p0, p1)
         for i, u in enumerate(units):
             for k in ((0, 1) if i == 0 else (i + 1,)):
                 if k < len(units):
                     if units[k].before is not None:
                         units[k].before()
-                    units[k].score(s_refs[k % 2])
-            u.soft(s_refs[i % 2], p_refs[i % 2])
+                    units[k].score(s_refs[k % 2], t_refs[k % 2])
+            u.soft(s_refs[i % 2], t_refs[i % 2], p_refs[i % 2])
             u.value(p_refs[i % 2])
 
         loads[4].wait()
@@ -369,48 +398,65 @@
         return pltpu.make_async_copy(hid_s.at[pl.ds(lo + shift, hi - lo)], ys_hbm.at[pl.ds(lo, hi - lo)], out_sem.at[p])
 
     def feed_forward(acc_s, u_s):
-        for p in range(PARTS):
-            r0, r1 = p * part, (p + 1) * part
-            if p == PARTS - 2:
+        def turn_step(turn, carry):
+            p, it = turn // n_part, lax.rem(turn, n_part)
+            r = pl.ds(pl.multiple_of(p * part, 16), part)
+
+            @pl.when(turn == (PARTS - 2) * n_part)
+            def _():
                 finish_global()
-            acc_s[...] = hid_s[r0:r1, :].astype(F32)
-            u_s[...] = jnp.zeros_like(u_s)
-
-            def step(i, carry):
-                t = p * n_tile + i
-                slot, prev = lax.rem(t, 3), lax.rem(t + 2, 3)
-                for c in w_copies(t, slot):
-                    c.wait()
-                s = mm(hid_s[r0:r1, :], w1_s[slot, :, :BLK])
-                acc_s[...] += mm(u_s[...], w2_s[prev, TILE - BLK:, :])
-                u = gelu(s).astype(BF16)
-                for c in range(BLK, TILE, BLK):
-                    s = mm(hid_s[r0:r1, :], w1_s[slot, :, c:c + BLK])
-                    acc_s[...] += mm(u, w2_s[slot, c - BLK:c, :])
-                    u = gelu(s).astype(BF16)
-                u_s[...] = u
-
-                @pl.when(t + 2 < PARTS * n_tile)
+
+            @pl.when(it == 0)
+            def _():
+                acc_s[...] = hid_s[r, :].astype(F32)
+                u_s[...] = jnp.zeros_like(u_s)
+
+            def chunk(j, u):
+                s = mm(hid_s[r, :], w1_s[:, j * BLK:(j + 1) * BLK])
+                k = (j - 1) % UNROLL
+                acc_s[...] += mm(u, w2_s[k * BLK:(k + 1) * BLK, :])
+                return gelu(s).astype(BF16)
+
+            u = u_s[...]
+            for c in (w1_copy(0, turn), w2_copy(2, turn), w2_copy(0, turn)):
+                c.wait()
+            for j in range(W1_CUT[0][1]):
+                u = chunk(j, u)
+            for c in (w1_copy(1, turn), w2_copy(1, turn)):
+                c.wait()
+            for c in (w1_copy(0, turn + 1), w2_copy(2, turn), w2_copy(0, turn + 1)):
+                c.start()
+            for j in range(W1_CUT[0][1], UNROLL):
+                u = chunk(j, u)
+            u_s[...] = u
+            for c in (w1_copy(1, turn + 1), w2_copy(1, turn + 1)):
+                c.start()
+
+            @pl.when(it == n_part - 1)
+            def _():
+                tail = w2_copy(2, turn)
+                tail.wait()
+                hid_s[r, :] = (acc_s[...] + mm(u_s[...], w2_s[(UNROLL - 1) * BLK:, :])).astype(BF16)
+                tail.start()
+
+            for q in range(PARTS):
+                @pl.when(turn == (q + 1) * n_part - 1)
                 def _():
-                    for c in w_copies(t + 2, prev):
-                        c.start()
-
-                return carry
-
-            lax.fori_loop(0, n_tile, step, 0)
-            slot = ((p + 1) * n_tile - 1) % 3
-            hid_s[r0:r1, :] = (acc_s[...] + mm(u_s[...], w2_s[slot, TILE - BLK:, :])).astype(BF16)
-            out_copy(p).start()
-            if p == PARTS - 2:
-                for k in range(1, n_dev):
-                    yg_copy(k, lax.rem(me + k, n_dev), me).start()
-                yg_s[pl.ds(me * per, per), :] = hid_s[split:split + per, :]
-
-    w2_s[2, TILE - BLK:, :] = jnp.zeros((BLK, dim), BF16)
+                    out_copy(q).start()
+                    if q == PARTS - 2:
+                        for k in range(1, n_dev):
+                            yg_copy(k, lax.rem(me + k, n_dev), me).start()
+                        yg_s[pl.ds(me * per, per), :] = hid_s[split:split + per, :]
+
+            return carry
+
+        lax.fori_loop(0, PARTS * n_part, turn_step, 0)
+
     pl.run_scoped(
         front,
         pltpu.VMEM((dim, heads * head), BF16), pltpu.VMEM((n_blk, stack, head), BF16), pltpu.VMEM((stack, ext), F32),
-        pltpu.VMEM((unit, rows), F32), pltpu.VMEM((unit, rows), F32), pltpu.VMEM((unit, rows), BF16), pltpu.VMEM((unit, rows), BF16),
+        pltpu.VMEM((unit, rows), F32), pltpu.VMEM((unit, rows), F32),
+        pltpu.VMEM((unit, 128), F32), pltpu.VMEM((unit, 128), F32), pltpu.VMEM((unit, rows), BF16), pltpu.VMEM((unit, rows), BF16),
         pltpu.VMEM((n_blk, stack, head), F32), pltpu.VMEM((n_blk, stack, 128), F32), pltpu.VMEM((n_blk, stack, 128), F32),
         pltpu.VMEM((unit, 128), F32), pltpu.VMEM((unit, 128), F32),
         pltpu.VMEM((rows, heads * head), BF16), pltpu.VMEM((n_dev * slab, head), BF16))
@@ -422,6 +468,8 @@
     last.start()
     for k in range(1, n_dev):
         yg_copy(k, lax.rem(me + k, n_dev), me).wait_send()
+    for c in first_weights():
+        c.wait()
     for p in range(PARTS):
         out_copy(p).wait()
     last.wait()
@@ -460,9 +508,9 @@
             pltpu.VMEM((n_dev * slab, head), F32), pltpu.VMEM((n_dev, slab, head), F32),
             pltpu.VMEM((n_dev, 8, slab), F32), pltpu.VMEM((n_dev, 8, slab), F32),
             pltpu.VMEM((rows + per, dim), BF16), pltpu.VMEM((n_glob, dim), BF16),
-            pltpu.VMEM((3, dim, TILE), BF16), pltpu.VMEM((3, TILE, dim), BF16),
+            pltpu.VMEM((dim, UNROLL * BLK), BF16), pltpu.VMEM((UNROLL * BLK, dim), BF16),
             dma((5,)), dma((6,)), dma((6,)), dma((4,)), dma((4,)), dma((n_dev,)), dma((n_dev,)), dma((n_dev,)), dma((n_dev,)),
-            dma((n_dev,)), dma((n_dev,)), dma((3,)), dma((3,)), dma((PARTS + 1,)),
+            dma((n_dev,)), dma((n_dev,)), dma((2,)), dma((3,)), dma((PARTS + 1,)),
         ],
         compiler_params=pltpu.CompilerParams(collective_id=0, has_side_effects=True, vmem_limit_bytes=67043328),
     )(x, wq, wk, wv, wo, w1, w2, rel_bias, gp)
@@ -471,8 +519,8 @@
 def place_kernel(ys_hbm, yg_hbm, gp_ref, y_hbm, yo_hbm, ys_s, y_s, yg_s, in_sem, out_sem):
     n = ys_s.shape[0]
     n_glob = gp_ref.shape[1]
-    gets = [pltpu.make_async_copy(ys_hbm.at[pl.ds(i * BLK, BLK)], ys_s.at[i], in_sem.at[i]) for i in range(n)]
-    puts = [pltpu.make_async_copy(y_s.at[i], y_hbm.at[pl.ds(i * BLK, BLK)], out_sem.at[i]) for i in range(n)]
+    gets = [pltpu.make_async_copy(ys_hbm.at[pl.ds(i * PIECE, PIECE)], ys_s.at[i], in_sem.at[i]) for i in range(n)]
+    puts = [pltpu.make_async_copy(y_s.at[i], y_hbm.at[pl.ds(i * PIECE, PIECE)], out_sem.at[i]) for i in range(n)]
     get_g = pltpu.make_async_copy(yg_hbm, yg_s, in_sem.at[n])
     put_g = pltpu.make_async_copy(yg_s, yo_hbm, out_sem.at[n])
     get_g.start()
@@ -481,8 +529,8 @@
     get_g.wait()
     put_g.start()
     for i in range(n):
-        first = (lax.axis_index('sp') * n + i) * BLK
-        hit = gp_ref[...] == first + lax.broadcasted_iota(jnp.int32, (BLK, n_glob), 0)
+        first = (lax.axis_index('sp') * n + i) * PIECE
+        hit = gp_ref[...] == first + lax.broadcasted_iota(jnp.int32, (PIECE, n_glob), 0)
         sel = hit.astype(F32)
         placed = mm(sel.astype(BF16), yg_s[...]).astype(BF16)
         is_glob = jnp.max(sel, axis=1, keepdims=True) > 0.0
@@ -496,7 +544,7 @@
 
 def place(ys, yg, gp):
     rows, dim = ys.shape
-    n = rows // BLK
+    n = rows // PIECE
     any_spec = pl.BlockSpec(memory_space=pl.ANY)
     dma = pltpu.SemaphoreType.DMA
     return pl.pallas_call(
@@ -505,7 +553,7 @@
         out_shape=(jax.ShapeDtypeStruct(ys.shape, BF16), jax.ShapeDtypeStruct(yg.shape, BF16)),
         in_specs=[any_spec, any_spec, pl.BlockSpec(memory_space=pltpu.VMEM)],
         out_specs=(any_spec, any_spec),
-        scratch_shapes=[pltpu.VMEM((n, BLK, dim), BF16), pltpu.VMEM((n, BLK, dim), BF16), pltpu.VMEM(yg.shape, BF16),
+        scratch_shapes=[pltpu.VMEM((n, PIECE, dim), BF16), pltpu.VMEM((n, PIECE, dim), BF16), pltpu.VMEM(yg.shape, BF16),
                         dma((n + 1,)), dma((n + 1,))],
         compiler_params=pltpu.CompilerParams(vmem_limit_bytes=60 << 20),
     )(ys, yg, gp)

time: 91.6 us -> 98.2 us (1.072)
  Pallas kernels: 90.6 us -> 97.2 us
    pallas_call x1, Pallas kernels: 86.1 us -> 92.2 us  [layer(): pl.pallas_call(functools.partial(layer_kernel, n_dev, heads, width), name...]
where the time goes in v4:
time: 98.2 us; the launch traced here: 98 us
  Pallas kernels  97.2 us (99%)
    pallas_call x1, Pallas kernels, layer(): pl.pallas_call(functools.partial(layer_kernel, n_dev, heads, width), name...  92.2 us
    pallas_call x1, Pallas kernels, place(): pl.pallas_call(place_kernel, name='place', out_shape=(jax.ShapeDtypeStruc...  4.91 us

profile of v4, /device:TPU:1, one launch (start us, length us, event | category | flops | bytes accessed | tf_op | source)
XLA Modules:
  0.0 98.0 jit_solution(13204110357672135923)
XLA Ops:
  0.6 92.2 %layer.1 = (bf16[1024,1152]{1,0:T(8,128)(2,1)}, bf16[256,1152]{1,0:T(8,128)(2,1)}) custom-call(bf16[1024,1152]{1,0:T(8,128)(2,1)} %x_hbm.1, bf16[1152,4,256]{2,1,0:T(4,128)(2,1)} %wq_hbm.1, bf16[1152,256]{1,0:T(8,128)(2,1)} %bitcast.5, bf16[1152,256]{1,0:T(8,128)(2,1)} %bitcast.6, bf16[1024,1152]{1,0:T(8,128)(2,1)} %bitcast.4, bf16[1152,6912]{1,0:T(8,128)(2,1)} %w1_hbm.1, ...), custom_call_target="tpu_custom_call" | custom-call | tf_op jit(solution)/shard_map/layer/pallas_call | solution.py:494
  92.9 4.9 %place.1 = (bf16[1024,1152]{1,0:T(8,128)(2,1)}, bf16[256,1152]{1,0:T(8,128)(2,1)}) custom-call(bf16[1024,1152]{1,0:T(8,128)(2,1)} %get-tuple-element.4.ys_hbm, bf16[256,1152]{1,0:T(8,128)(2,1)} %get-tuple-element.5.yg_hbm, s32[1,256]{1,0:T(1,128)} %bitcast.8), custom_call_target="tpu_custom_call" | custom-call | tf_op jit(solution)/shard_map/place/pallas_call | solution.py:550

commit v5 on v4

--- a/solution.py
+++ b/solution.py
@@ -13,11 +13,11 @@
 NEG = -math.inf
 BLK = 256
 ROW = 32
-PIECE = 128
+PIECE = 256
 PARTS = 3
 UNROLL = 9
-W1_CUT = ((0, 5), (5, 4))
-W2_CUT = ((0, 4), (4, 4), (8, 1))
+W1_CUT = ((0, 3), (3, 3), (6, 3))
+W2_CUT = ((0, 2), (2, 3), (5, 3), (8, 1))
 
 
 def mm(a, b):
@@ -103,8 +103,10 @@
         at = lax.rem(turn, n_part) * (UNROLL * BLK) + lo * BLK
         return pltpu.make_async_copy(w2_hbm.at[pl.ds(at, n * BLK), :], w2_s.at[pl.ds(lo * BLK, n * BLK), :], w2_sem.at[i])
 
-    def first_weights():
-        return [w1_copy(0, 0), w2_copy(2, 0), w2_copy(0, 0), w1_copy(1, 0), w2_copy(1, 0)]
+    def group(k, turn):
+        if k == 0:
+            return [w1_copy(0, turn), w2_copy(3, turn - 1), w2_copy(0, turn)]
+        return [w1_copy(k, turn), w2_copy(k, turn)]
 
     def rs_copies(k):
         peer = lax.rem(me + k, n_dev)
@@ -156,8 +158,9 @@
                            halo_ssem.at[sem + i], halo_rsem.at[sem + i], peer) for i in range(2)]
 
         loads[4].start()
-        for c in first_weights():
-            c.start()
+        for k in range(3):
+            for c in group(k, n_part):
+                c.start()
         to_near = halo_copies(near, core, partner, 0)
         to_far = halo_copies(far, 1 - core, far_peer, 2)
         for c in to_near:
@@ -418,26 +421,21 @@
                 return gelu(s).astype(BF16)
 
             u = u_s[...]
-            for c in (w1_copy(0, turn), w2_copy(2, turn), w2_copy(0, turn)):
-                c.wait()
-            for j in range(W1_CUT[0][1]):
+            for j in range(UNROLL):
+                if j % 3 == 2:
+                    k = (j + 1) // 3 % 3
+                    for c in group(k, turn + (k == 0)):
+                        c.wait()
                 u = chunk(j, u)
-            for c in (w1_copy(1, turn), w2_copy(1, turn)):
-                c.wait()
-            for c in (w1_copy(0, turn + 1), w2_copy(2, turn), w2_copy(0, turn + 1)):
-                c.start()
-            for j in range(W1_CUT[0][1], UNROLL):
-                u = chunk(j, u)
+                if j % 3 == 2:
+                    k = j // 3
+                    for c in group(k, turn + 1):
+                        c.start()
             u_s[...] = u
-            for c in (w1_copy(1, turn + 1), w2_copy(1, turn + 1)):
-                c.start()
 
             @pl.when(it == n_part - 1)
             def _():
-                tail = w2_copy(2, turn)
-                tail.wait()
                 hid_s[r, :] = (acc_s[...] + mm(u_s[...], w2_s[(UNROLL - 1) * BLK:, :])).astype(BF16)
-                tail.start()
 
             for q in range(PARTS):
                 @pl.when(turn == (q + 1) * n_part - 1)
@@ -450,6 +448,8 @@
 
             return carry
 
+        for c in group(0, n_part):
+            c.wait()
         lax.fori_loop(0, PARTS * n_part, turn_step, 0)
 
     pl.run_scoped(
@@ -468,8 +468,9 @@
     last.start()
     for k in range(1, n_dev):
         yg_copy(k, lax.rem(me + k, n_dev), me).wait_send()
-    for c in first_weights():
-        c.wait()
+    for k in (1, 2):
+        for c in group(k, 0):
+            c.wait()
     for p in range(PARTS):
         out_copy(p).wait()
     last.wait()
@@ -510,7 +511,7 @@
             pltpu.VMEM((rows + per, dim), BF16), pltpu.VMEM((n_glob, dim), BF16),
             pltpu.VMEM((dim, UNROLL * BLK), BF16), pltpu.VMEM((UNROLL * BLK, dim), BF16),
             dma((5,)), dma((6,)), dma((6,)), dma((4,)), dma((4,)), dma((n_dev,)), dma((n_dev,)), dma((n_dev,)), dma((n_dev,)),
-            dma((n_dev,)), dma((n_dev,)), dma((2,)), dma((3,)), dma((PARTS + 1,)),
+            dma((n_dev,)), dma((n_dev,)), dma((3,)), dma((4,)), dma((PARTS + 1,)),
         ],
         compiler_params=pltpu.CompilerParams(collective_id=0, has_side_effects=True, vmem_limit_bytes=67043328),
     )(x, wq, wk, wv, wo, w1, w2, rel_bias, gp)

time: 98.2 us -> 94 us (0.957)
  Pallas kernels: 97.2 us -> 93 us
    pallas_call x1, Pallas kernels: 92.2 us -> 88.5 us  [layer(): pl.pallas_call(functools.partial(layer_kernel, n_dev, heads, width), name...]
where the time goes in v5:
time: 94 us; the launch traced here: 93.8 us
  Pallas kernels  93 us (99%)
    pallas_call x1, Pallas kernels, layer(): pl.pallas_call(functools.partial(layer_kernel, n_dev, heads, width), name...  88.5 us
    pallas_call x1, Pallas kernels, place(): pl.pallas_call(place_kernel, name='place', out_shape=(jax.ShapeDtypeStruc...  4.5 us

profile of v5, /device:TPU:1, one launch (start us, length us, event | category | flops | bytes accessed | tf_op | source)
XLA Modules:
  0.0 93.8 jit_solution(2046260044410967532)
XLA Ops:
  0.6 88.5 %layer.1 = (bf16[1024,1152]{1,0:T(8,128)(2,1)}, bf16[256,1152]{1,0:T(8,128)(2,1)}) custom-call(bf16[1024,1152]{1,0:T(8,128)(2,1)} %x_hbm.1, bf16[1152,4,256]{2,1,0:T(4,128)(2,1)} %wq_hbm.1, bf16[1152,256]{1,0:T(8,128)(2,1)} %bitcast.5, bf16[1152,256]{1,0:T(8,128)(2,1)} %bitcast.6, bf16[1024,1152]{1,0:T(8,128)(2,1)} %bitcast.4, bf16[1152,6912]{1,0:T(8,128)(2,1)} %w1_hbm.1, ...), custom_call_target="tpu_custom_call" | custom-call | tf_op jit(solution)/shard_map/layer/pallas_call | solution.py:495
  89.2 4.5 %place.1 = (bf16[1024,1152]{1,0:T(8,128)(2,1)}, bf16[256,1152]{1,0:T(8,128)(2,1)}) custom-call(bf16[1024,1152]{1,0:T(8,128)(2,1)} %get-tuple-element.4.ys_hbm, bf16[256,1152]{1,0:T(8,128)(2,1)} %get-tuple-element.5.yg_hbm, s32[1,256]{1,0:T(1,128)} %bitcast.8), custom_call_target="tpu_custom_call" | custom-call | tf_op jit(solution)/shard_map/place/pallas_call | solution.py:551

commit v6 on v5

--- a/solution.py
+++ b/solution.py
@@ -15,9 +15,7 @@
 ROW = 32
 PIECE = 256
 PARTS = 3
-UNROLL = 9
-W1_CUT = ((0, 3), (3, 3), (6, 3))
-W2_CUT = ((0, 2), (2, 3), (5, 3), (8, 1))
+TILE = 768
 
 
 def mm(a, b):
@@ -64,13 +62,12 @@
 
 def layer_kernel(n_dev, heads, width,
                  x_hbm, wq_hbm, wk_hbm, wv_hbm, wo_hbm, w1_hbm, w2_hbm, rb_ref, gp_ref, ys_hbm, yg_hbm,
-                 x_s, wq3_s, wk_s, wv_s, wo_s, kv_s, halo_s, row_s, mask_s,
-                 xg_send, xp_recv, xh_s, xa_recv, xh2_s, xb_recv, xg_all, rs_send, rs_recv, st_send, st_recv,
-                 hid_s, yg_s, w1_s, w2_s,
+                 x_s, wo_s, halo_s, row_s, mask_s, xp_recv, xa_recv, xb_recv, xg_all, rs_send, rs_recv, st_send, st_recv,
+                 hid_s, yg_s, att_s,
                  in_sem, x_ssem, x_rsem, halo_ssem, halo_rsem, rs_ssem, rs_rsem, st_ssem, st_rsem, yg_ssem, yg_rsem,
                  w1_sem, w2_sem, out_sem):
     rows, dim = x_s.shape
-    head = wk_s.shape[1]
+    head = wk_hbm.shape[1]
     n_glob = gp_ref.shape[1]
     per = n_glob // n_dev
     slab = heads * per
@@ -80,7 +77,7 @@
     ext = BLK + 2 * width
     part = (rows + per) // PARTS
     split = part * (PARTS - 1) - per
-    n_chunk = w1_hbm.shape[1] // BLK
+    n_tile = w1_hbm.shape[1] // TILE
     me = lax.axis_index('sp')
     start = me * rows
     core = lax.rem(me, 2)
@@ -91,29 +88,12 @@
     half = n_glob // 2
     quart = n_glob // 4
 
-    n_part = n_chunk // UNROLL
-
-    def w1_copy(i, turn):
-        lo, n = W1_CUT[i]
-        at = lax.rem(turn, n_part) * (UNROLL * BLK) + lo * BLK
-        return pltpu.make_async_copy(w1_hbm.at[:, pl.ds(at, n * BLK)], w1_s.at[:, pl.ds(lo * BLK, n * BLK)], w1_sem.at[i])
-
-    def w2_copy(i, turn):
-        lo, n = W2_CUT[i]
-        at = lax.rem(turn, n_part) * (UNROLL * BLK) + lo * BLK
-        return pltpu.make_async_copy(w2_hbm.at[pl.ds(at, n * BLK), :], w2_s.at[pl.ds(lo * BLK, n * BLK), :], w2_sem.at[i])
-
-    def group(k, turn):
-        if k == 0:
-            return [w1_copy(0, turn), w2_copy(3, turn - 1), w2_copy(0, turn)]
-        return [w1_copy(k, turn), w2_copy(k, turn)]
-
     def rs_copies(k):
         peer = lax.rem(me + k, n_dev)
         return (remote(rs_send.at[pl.ds(peer * slab, slab)], rs_recv.at[k], rs_ssem.at[k], rs_rsem.at[k], peer),
                 remote(st_send.at[peer], st_recv.at[k], st_ssem.at[k], st_rsem.at[k], peer))
 
-    def front(wq_s, q_s, bias_s, s0, s1, t0, t1, p0, p1, o_s, m_s, l_s, mg_s, lg_s, att_s, qg_s):
+    def front(wq3_s, wq_s, wk_s, wv_s, kv_s, xg_send, xh_s, xh2_s, q_s, bias_s, s0, s1, t0, t1, p0, p1, o_s, m_s, l_s, mg_s, lg_s, qg_s):
         loads = [pltpu.make_async_copy(src, dst, in_sem.at[i]) for i, (src, dst) in enumerate(
             [(x_hbm, x_s), (wk_hbm, wk_s), (wv_hbm, wv_s), (wq_hbm, wq3_s), (wo_hbm, wo_s)])]
         for c in loads[:3]:
@@ -158,9 +138,6 @@
                            halo_ssem.at[sem + i], halo_rsem.at[sem + i], peer) for i in range(2)]
 
         loads[4].start()
-        for k in range(3):
-            for c in group(k, n_part):
-                c.start()
         to_near = halo_copies(near, core, partner, 0)
         to_far = halo_copies(far, 1 - core, far_peer, 2)
         for c in to_near:
@@ -350,16 +327,6 @@
                     units[k].score(s_refs[k % 2], t_refs[k % 2])
             u.soft(s_refs[i % 2], t_refs[i % 2], p_refs[i % 2])
             u.value(p_refs[i % 2])
-
-        loads[4].wait()
-        for b in range(n_blk):
-            r0, r1 = b * BLK, (b + 1) * BLK
-            res = (x_s[r0:r1, :].astype(F32) + mm(att_s[r0:r1, :], wo_s[...])).astype(BF16)
-            cut = min(max(split - r0, 0), BLK)
-            if cut:
-                hid_s[r0:r0 + cut, :] = res[:cut]
-            if cut < BLK:
-                hid_s[r0 + cut + per:r1 + per, :] = res[cut:]
 
         for c in [pair] + swap + swap2 + [spread] + to_near:
             c.wait_send()
@@ -400,67 +367,68 @@
         shift = per if p == PARTS - 1 else 0
         return pltpu.make_async_copy(hid_s.at[pl.ds(lo + shift, hi - lo)], ys_hbm.at[pl.ds(lo, hi - lo)], out_sem.at[p])
 
-    def feed_forward(acc_s, u_s):
-        def turn_step(turn, carry):
-            p, it = turn // n_part, lax.rem(turn, n_part)
-            r = pl.ds(pl.multiple_of(p * part, 16), part)
-
-            @pl.when(turn == (PARTS - 2) * n_part)
-            def _():
+    def feed_forward(acc_s, u_s, w1_s, w2_s):
+        def w_copies(i):
+            at = pl.ds(i * TILE, TILE)
+            return (pltpu.make_async_copy(w1_hbm.at[:, at], w1_s.at[i], w1_sem.at[i]),
+                    pltpu.make_async_copy(w2_hbm.at[at, :], w2_s.at[i], w2_sem.at[i]))
+
+        for i in range(n_tile):
+            for c in w_copies(i):
+                c.start()
+
+        pltpu.make_async_copy(wo_hbm, wo_s, in_sem.at[4]).wait()
+        for b in range(n_blk):
+            r0, r1 = b * BLK, (b + 1) * BLK
+            res = (x_s[r0:r1, :].astype(F32) + mm(att_s[r0:r1, :], wo_s[...])).astype(BF16)
+            cut = min(max(split - r0, 0), BLK)
+            if cut:
+                hid_s[r0:r0 + cut, :] = res[:cut]
+            if cut < BLK:
+                hid_s[r0 + cut + per:r1 + per, :] = res[cut:]
+
+        for p in range(PARTS):
+            r0, r1 = p * part, (p + 1) * part
+            if p == PARTS - 2:
                 finish_global()
-
-            @pl.when(it == 0)
-            def _():
-                acc_s[...] = hid_s[r, :].astype(F32)
-                u_s[...] = jnp.zeros_like(u_s)
-
-            def chunk(j, u):
-                s = mm(hid_s[r, :], w1_s[:, j * BLK:(j + 1) * BLK])
-                k = (j - 1) % UNROLL
-                acc_s[...] += mm(u, w2_s[k * BLK:(k + 1) * BLK, :])
-                return gelu(s).astype(BF16)
-
-            u = u_s[...]
-            for j in range(UNROLL):
-                if j % 3 == 2:
-                    k = (j + 1) // 3 % 3
-                    for c in group(k, turn + (k == 0)):
+            acc_s[...] = hid_s[r0:r1, :].astype(F32)
+            u_s[...] = jnp.zeros_like(u_s)
+
+            def step(i, carry):
+                if p == 0:
+                    for c in w_copies(i):
                         c.wait()
-                u = chunk(j, u)
-                if j % 3 == 2:
-                    k = j // 3
-                    for c in group(k, turn + 1):
-                        c.start()
-            u_s[...] = u
-
-            @pl.when(it == n_part - 1)
-            def _():
-                hid_s[r, :] = (acc_s[...] + mm(u_s[...], w2_s[(UNROLL - 1) * BLK:, :])).astype(BF16)
-
-            for q in range(PARTS):
-                @pl.when(turn == (q + 1) * n_part - 1)
-                def _():
-                    out_copy(q).start()
-                    if q == PARTS - 2:
-                        for k in range(1, n_dev):
-                            yg_copy(k, lax.rem(me + k, n_dev), me).start()
-                        yg_s[pl.ds(me * per, per), :] = hid_s[split:split + per, :]
-
-            return carry
-
-        for c in group(0, n_part):
-            c.wait()
-        lax.fori_loop(0, PARTS * n_part, turn_step, 0)
+                before = jnp.maximum(i - 1, 0)
+                s = mm(hid_s[r0:r1, :], w1_s[i, :, :BLK])
+                acc_s[...] += mm(u_s[...], w2_s[before, TILE - BLK:, :])
+                u = gelu(s).astype(BF16)
+                for c in range(BLK, TILE, BLK):
+                    s = mm(hid_s[r0:r1, :], w1_s[i, :, c:c + BLK])
+                    acc_s[...] += mm(u, w2_s[i, c - BLK:c, :])
+                    u = gelu(s).astype(BF16)
+                u_s[...] = u
+                return carry
+
+            lax.fori_loop(0, n_tile, step, 0)
+            hid_s[r0:r1, :] = (acc_s[...] + mm(u_s[...], w2_s[n_tile - 1, TILE - BLK:, :])).astype(BF16)
+            out_copy(p).start()
+            if p == PARTS - 2:
+                for k in range(1, n_dev):
+                    yg_copy(k, lax.rem(me + k, n_dev), me).start()
+                yg_s[pl.ds(me * per, per), :] = hid_s[split:split + per, :]
 
     pl.run_scoped(
         front,
-        pltpu.VMEM((dim, heads * head), BF16), pltpu.VMEM((n_blk, stack, head), BF16), pltpu.VMEM((stack, ext), F32),
-        pltpu.VMEM((unit, rows), F32), pltpu.VMEM((unit, rows), F32),
-        pltpu.VMEM((unit, 128), F32), pltpu.VMEM((unit, 128), F32), pltpu.VMEM((unit, rows), BF16), pltpu.VMEM((unit, rows), BF16),
+        pltpu.VMEM(wq_hbm.shape, BF16), pltpu.VMEM((dim, heads * head), BF16), pltpu.VMEM((dim, head), BF16), pltpu.VMEM((dim, head), BF16),
+        pltpu.VMEM((rows, 2 * head), BF16),
+        pltpu.VMEM((n_glob, dim), BF16), pltpu.VMEM((half, dim), BF16), pltpu.VMEM((half, dim), BF16),
+        pltpu.VMEM((n_blk, stack, head), BF16), pltpu.VMEM((stack, ext), F32),
+        pltpu.VMEM((unit, rows), F32), pltpu.VMEM((unit, rows), F32), pltpu.VMEM((unit, 128), F32), pltpu.VMEM((unit, 128), F32),
+        pltpu.VMEM((unit, rows), BF16), pltpu.VMEM((unit, rows), BF16),
         pltpu.VMEM((n_blk, stack, head), F32), pltpu.VMEM((n_blk, stack, 128), F32), pltpu.VMEM((n_blk, stack, 128), F32),
-        pltpu.VMEM((unit, 128), F32), pltpu.VMEM((unit, 128), F32),
-        pltpu.VMEM((rows, heads * head), BF16), pltpu.VMEM((n_dev * slab, head), BF16))
-    pl.run_scoped(feed_forward, pltpu.VMEM((part, dim), F32), pltpu.VMEM((part, BLK), BF16))
+        pltpu.VMEM((unit, 128), F32), pltpu.VMEM((unit, 128), F32), pltpu.VMEM((n_dev * slab, head), BF16))
+    pl.run_scoped(feed_forward, pltpu.VMEM((part, dim), F32), pltpu.VMEM((part, BLK), BF16),
+                  pltpu.VMEM((n_tile, dim, TILE), BF16), pltpu.VMEM((n_tile, TILE, dim), BF16))
     for k in range(1, n_dev):
         src = lax.rem(me + n_dev - k, n_dev)
         yg_copy(k, src, src).wait_recv()
@@ -468,9 +436,6 @@
     last.start()
     for k in range(1, n_dev):
         yg_copy(k, lax.rem(me + k, n_dev), me).wait_send()
-    for k in (1, 2):
-        for c in group(k, 0):
-            c.wait()
     for p in range(PARTS):
         out_copy(p).wait()
     last.wait()
@@ -499,19 +464,15 @@
         in_specs=[any_spec] * 7 + [vmem_spec] * 2,
         out_specs=(any_spec, any_spec),
         scratch_shapes=[
-            pltpu.VMEM(x.shape, BF16), pltpu.VMEM(wq.shape, BF16), pltpu.VMEM(wk.shape, BF16),
-            pltpu.VMEM(wv.shape, BF16), pltpu.VMEM(wo.shape, BF16),
-            pltpu.VMEM((rows, 2 * head), BF16), pltpu.VMEM((2, 3 * BLK, 2 * head), BF16),
+            pltpu.VMEM(x.shape, BF16), pltpu.VMEM(wo.shape, BF16), pltpu.VMEM((2, 3 * BLK, 2 * head), BF16),
             pltpu.VMEM((8, BLK + 2 * width), F32), pltpu.VMEM((8, rows + 2 * width), F32),
-            pltpu.VMEM((n_glob, dim), BF16), pltpu.VMEM((n_glob // 2, dim), BF16), pltpu.VMEM((n_glob // 2, dim), BF16),
-            pltpu.VMEM((2, n_glob // 4, dim), BF16), pltpu.VMEM((n_glob // 2, dim), BF16), pltpu.VMEM((2, n_glob // 4, dim), BF16),
+            pltpu.VMEM((n_glob // 2, dim), BF16), pltpu.VMEM((2, n_glob // 4, dim), BF16), pltpu.VMEM((2, n_glob // 4, dim), BF16),
             pltpu.VMEM((n_glob, dim), BF16),
             pltpu.VMEM((n_dev * slab, head), F32), pltpu.VMEM((n_dev, slab, head), F32),
             pltpu.VMEM((n_dev, 8, slab), F32), pltpu.VMEM((n_dev, 8, slab), F32),
-            pltpu.VMEM((rows + per, dim), BF16), pltpu.VMEM((n_glob, dim), BF16),
-            pltpu.VMEM((dim, UNROLL * BLK), BF16), pltpu.VMEM((UNROLL * BLK, dim), BF16),
+            pltpu.VMEM((rows + per, dim), BF16), pltpu.VMEM((n_glob, dim), BF16), pltpu.VMEM((rows, heads * head), BF16),
             dma((5,)), dma((6,)), dma((6,)), dma((4,)), dma((4,)), dma((n_dev,)), dma((n_dev,)), dma((n_dev,)), dma((n_dev,)),
-            dma((n_dev,)), dma((n_dev,)), dma((3,)), dma((4,)), dma((PARTS + 1,)),
+            dma((n_dev,)), dma((n_dev,)), dma((w1.shape[1] // TILE,)), dma((w1.shape[1] // TILE,)), dma((PARTS + 1,)),
         ],
         compiler_params=pltpu.CompilerParams(collective_id=0, has_side_effects=True, vmem_limit_bytes=67043328),
     )(x, wq, wk, wv, wo, w1, w2, rel_bias, gp)

time: 94 us -> 91 us (0.968)
  Pallas kernels: 93 us -> 90 us
    pallas_call x1, Pallas kernels: 88.5 us -> 85.5 us  [layer(): pl.pallas_call(functools.partial(layer_kernel, n_dev, heads, width), name...]
where the time goes in v6:
time: 91 us; the launch traced here: 90.8 us
  Pallas kernels  90 us (99%)
    pallas_call x1, Pallas kernels, layer(): pl.pallas_call(functools.partial(layer_kernel, n_dev, heads, width), name...  85.5 us
    pallas_call x1, Pallas kernels, place(): pl.pallas_call(place_kernel, name='place', out_shape=(jax.ShapeDtypeStruc...  4.5 us

profile of v6, /device:TPU:1, one launch (start us, length us, event | category | flops | bytes accessed | tf_op | source)
XLA Modules:
  0.0 90.8 jit_solution(9362292169927763182)
XLA Ops:
  0.6 85.5 %layer.1 = (bf16[1024,1152]{1,0:T(8,128)(2,1)}, bf16[256,1152]{1,0:T(8,128)(2,1)}) custom-call(bf16[1024,1152]{1,0:T(8,128)(2,1)} %x_hbm.1, bf16[1152,4,256]{2,1,0:T(4,128)(2,1)} %wq_hbm.1, bf16[1152,256]{1,0:T(8,128)(2,1)} %bitcast.5, bf16[1152,256]{1,0:T(8,128)(2,1)} %bitcast.6, bf16[1024,1152]{1,0:T(8,128)(2,1)} %bitcast.4, bf16[1152,6912]{1,0:T(8,128)(2,1)} %w1_hbm.1, ...), custom_call_target="tpu_custom_call" | custom-call | tf_op jit(solution)/shard_map/layer/pallas_call | solution.py:460
  86.1 4.5 %place.1 = (bf16[1024,1152]{1,0:T(8,128)(2,1)}, bf16[256,1152]{1,0:T(8,128)(2,1)}) custom-call(bf16[1024,1152]{1,0:T(8,128)(2,1)} %get-tuple-element.4.ys_hbm, bf16[256,1152]{1,0:T(8,128)(2,1)} %get-tuple-element.5.yg_hbm, s32[1,256]{1,0:T(1,128)} %bitcast.8), custom_call_target="tpu_custom_call" | custom-call | tf_op jit(solution)/shard_map/place/pallas_call | solution.py:512

commit v7 on v6

--- a/solution.py
+++ b/solution.py
@@ -16,6 +16,7 @@
 PIECE = 256
 PARTS = 3
 TILE = 768
+WIDE = 3
 
 
 def mm(a, b):
@@ -32,11 +33,11 @@
         device_id={'sp': dev}, device_id_type=pl.DeviceIdType.MESH)
 
 
-def entry_barrier(me, n_dev):
+def announce(me, n_dev):
     barrier = pltpu.get_barrier_semaphore()
     for k in range(1, n_dev):
         pl.semaphore_signal(barrier, inc=1, device_id={'sp': lax.rem(me + k, n_dev)}, device_id_type=pl.DeviceIdType.MESH)
-    pl.semaphore_wait(barrier, n_dev - 1)
+    return barrier
 
 
 def diagonal(n):
@@ -98,7 +99,7 @@
             [(x_hbm, x_s), (wk_hbm, wk_s), (wv_hbm, wv_s), (wq_hbm, wq3_s), (wo_hbm, wo_s)])]
         for c in loads[:3]:
             c.start()
-        entry_barrier(me, n_dev)
+        barrier = announce(me, n_dev)
 
         gp_col = row_to_column(gp_ref[...].astype(F32)).astype(jnp.int32)
         own = gp_col == start + lax.broadcasted_iota(jnp.int32, (n_glob, rows), 1)
@@ -121,6 +122,7 @@
 
         xg_send[...] = mm(own.astype(F32).astype(BF16), x).astype(BF16)
         pair = remote(xg_send.at[pl.ds((1 - core) * half, half)], xp_recv, x_ssem.at[0], x_rsem.at[0], partner)
+        pl.semaphore_wait(barrier, n_dev - 1)
         pair.start()
 
         loads[1].wait()
@@ -133,8 +135,8 @@
         far_peer = lax.rem(me + n_dev - 1 + 2 * core, n_dev)
 
         def halo_copies(mine, theirs, peer, sem):
-            return [remote(kv_s.at[pl.ds(mine * width + i * BLK, BLK)],
-                           halo_s.at[theirs, pl.ds((i + theirs - 2 * i * theirs) * BLK, BLK)],
+            return [remote(kv_s.at[pl.ds(mine * width + (i + theirs - 2 * i * theirs) * BLK, BLK)],
+                           halo_s.at[theirs, pl.ds(i * BLK, BLK)],
                            halo_ssem.at[sem + i], halo_rsem.at[sem + i], peer) for i in range(2)]
 
         loads[4].start()
@@ -270,7 +272,7 @@
 
             @pl.when(has_far)
             def _():
-                for c in to_far:
+                for c in to_far[::-1]:
                     c.start()
 
             @pl.when(jnp.logical_not(has_far))
@@ -302,22 +304,25 @@
             for c in to_near:
                 c.wait_recv()
 
-        def start_partials():
+        def wait_far(i):
+            @pl.when(has_far)
+            def _():
+                to_far[i].wait_recv()
+
+        def inner_ready():
+            wait_far(1)
+
+        def outer_ready():
+            wait_far(0)
             for k in range(1, n_dev):
                 for c in rs_copies(k):
                     c.start()
 
-        def wait_far():
-            @pl.when(has_far)
-            def _():
-                for c in to_far:
-                    c.wait_recv()
-
         hooks = {2: second_swap, 7: share}
         units = [Local(i // 2, i % 2, hooks.get(i)) for i in range(2 * n_blk)]
         units += [Global(0, project_global), Global(1)]
-        units += [Far(near, False, 0, near_ready), Far(near, False, 1, start_partials), Far(near, True, 0), Far(near, True, 1)]
-        units += [Far(far, False, 0, wait_far), Far(far, False, 1), Far(far, True, 0), Far(far, True, 1)]
+        units += [Far(near, False, 0, near_ready), Far(near, False, 1), Far(near, True, 0), Far(near, True, 1)]
+        units += [Far(far, True, 0, inner_ready), Far(far, True, 1), Far(far, False, 0, outer_ready), Far(far, False, 1)]
         s_refs, t_refs, p_refs = (s0, s1), (t0, t1), (p0, p1)
         for i, u in enumerate(units):
             for k in ((0, 1) if i == 0 else (i + 1,)):
@@ -387,35 +392,59 @@
             if cut < BLK:
                 hid_s[r0 + cut + per:r1 + per, :] = res[cut:]
 
-        for p in range(PARTS):
-            r0, r1 = p * part, (p + 1) * part
-            if p == PARTS - 2:
-                finish_global()
-            acc_s[...] = hid_s[r0:r1, :].astype(F32)
+        def chunks(r, i, count):
+            u = u_s[...]
+            for c in range(count):
+                g, at = i + c // (TILE // BLK), c % (TILE // BLK) * BLK
+                s = mm(hid_s[r, :], w1_s[g, :, at:at + BLK])
+                if c == 0:
+                    acc_s[...] += mm(u, w2_s[jnp.maximum(i - 1, 0), TILE - BLK:, :])
+                else:
+                    b = c - 1
+                    at = b % (TILE // BLK) * BLK
+                    acc_s[...] += mm(u, w2_s[i + b // (TILE // BLK), at:at + BLK, :])
+                u = gelu(s).astype(BF16)
+            u_s[...] = u
+
+        def run_part(r, steps, step):
+            acc_s[...] = hid_s[r, :].astype(F32)
             u_s[...] = jnp.zeros_like(u_s)
+            lax.fori_loop(0, steps, step, 0)
+            hid_s[r, :] = (acc_s[...] + mm(u_s[...], w2_s[n_tile - 1, TILE - BLK:, :])).astype(BF16)
+
+        def first(i, carry):
+            for c in w_copies(i):
+                c.wait()
+            chunks(slice(0, part), i, TILE // BLK)
+            return carry
+
+        run_part(slice(0, part), n_tile, first)
+        out_copy(0).start()
+        finish_global()
+
+        def later(p, carry):
+            r = pl.ds(pl.multiple_of(p * part, 16), part)
 
             def step(i, carry):
-                if p == 0:
-                    for c in w_copies(i):
-                        c.wait()
-                before = jnp.maximum(i - 1, 0)
-                s = mm(hid_s[r0:r1, :], w1_s[i, :, :BLK])
-                acc_s[...] += mm(u_s[...], w2_s[before, TILE - BLK:, :])
-                u = gelu(s).astype(BF16)
-                for c in range(BLK, TILE, BLK):
-                    s = mm(hid_s[r0:r1, :], w1_s[i, :, c:c + BLK])
-                    acc_s[...] += mm(u, w2_s[i, c - BLK:c, :])
-                    u = gelu(s).astype(BF16)
-                u_s[...] = u
+                chunks(r, i * WIDE, WIDE * (TILE // BLK))
                 return carry
 
-            lax.fori_loop(0, n_tile, step, 0)
-            hid_s[r0:r1, :] = (acc_s[...] + mm(u_s[...], w2_s[n_tile - 1, TILE - BLK:, :])).astype(BF16)
-            out_copy(p).start()
-            if p == PARTS - 2:
+            run_part(r, n_tile // WIDE, step)
+
+            @pl.when(p == PARTS - 2)
+            def _():
                 for k in range(1, n_dev):
                     yg_copy(k, lax.rem(me + k, n_dev), me).start()
                 yg_s[pl.ds(me * per, per), :] = hid_s[split:split + per, :]
+
+            for q in range(1, PARTS):
+                @pl.when(p == q)
+                def _():
+                    out_copy(q).start()
+
+            return carry
+
+        lax.fori_loop(1, PARTS, later, 0)
 
     pl.run_scoped(
         front,

time: 91 us -> 85 us (0.934)
  the two profiles are of different devices: /device:TPU:1 before, /device:TPU:0 now
where the time goes in v7:
time: 85 us; the launch traced here: 84 us
  Pallas kernels  83.2 us (98%)
    pallas_call x1, Pallas kernels, layer(): pl.pallas_call(functools.partial(layer_kernel, n_dev, heads, width), name...  78.7 us
    pallas_call x1, Pallas kernels, place(): pl.pallas_call(place_kernel, name='place', out_shape=(jax.ShapeDtypeStruc...  4.5 us

profile of v7, /device:TPU:0, one launch (start us, length us, event | category | flops | bytes accessed | tf_op | source)
XLA Modules:
  0.0 84.0 jit_solution(10196852387354541435)
XLA Ops:
  0.6 78.7 %layer.1 = (bf16[1024,1152]{1,0:T(8,128)(2,1)}, bf16[256,1152]{1,0:T(8,128)(2,1)}) custom-call(bf16[1024,1152]{1,0:T(8,128)(2,1)} %x_hbm.1, bf16[1152,4,256]{2,1,0:T(4,128)(2,1)} %wq_hbm.1, bf16[1152,256]{1,0:T(8,128)(2,1)} %bitcast.5, bf16[1152,256]{1,0:T(8,128)(2,1)} %bitcast.6, bf16[1024,1152]{1,0:T(8,128)(2,1)} %bitcast.4, bf16[1152,6912]{1,0:T(8,128)(2,1)} %w1_hbm.1, ...), custom_call_target="tpu_custom_call" | custom-call | tf_op jit(solution)/shard_map/layer/pallas_call | solution.py:489
  79.4 4.5 %place.1 = (bf16[1024,1152]{1,0:T(8,128)(2,1)}, bf16[256,1152]{1,0:T(8,128)(2,1)}) custom-call(bf16[1024,1152]{1,0:T(8,128)(2,1)} %get-tuple-element.4.ys_hbm, bf16[256,1152]{1,0:T(8,128)(2,1)} %get-tuple-element.5.yg_hbm, s32[1,256]{1,0:T(1,128)} %bitcast.8), custom_call_target="tpu_custom_call" | custom-call | tf_op jit(solution)/shard_map/place/pallas_call | solution.py:541

commit v8 on v7

--- a/solution.py
+++ b/solution.py
@@ -134,19 +134,20 @@
         has_far = (me > 0) & (me < n_dev - 1)
         far_peer = lax.rem(me + n_dev - 1 + 2 * core, n_dev)
 
-        def halo_copies(mine, theirs, peer, sem):
-            return [remote(kv_s.at[pl.ds(mine * width + (i + theirs - 2 * i * theirs) * BLK, BLK)],
-                           halo_s.at[theirs, pl.ds(i * BLK, BLK)],
-                           halo_ssem.at[sem + i], halo_rsem.at[sem + i], peer) for i in range(2)]
+        def halo_copies(mine, theirs, peer, sem, pieces):
+            out = []
+            for k, (at, size) in enumerate(pieces):
+                blk = at // BLK + theirs - 2 * (at // BLK) * theirs
+                out.append(remote(kv_s.at[pl.ds(mine * width + blk * BLK + at % BLK, size)], halo_s.at[theirs, pl.ds(at, size)],
+                                  halo_ssem.at[sem + k], halo_rsem.at[sem + k], peer))
+            return out
 
         loads[4].start()
-        to_near = halo_copies(near, core, partner, 0)
-        to_far = halo_copies(far, 1 - core, far_peer, 2)
+        to_near = halo_copies(near, core, partner, 0, ((0, BLK), (BLK, BLK)))
+        to_far = halo_copies(far, 1 - core, far_peer, 2, ((0, BLK), (BLK, BLK // 2), (BLK + BLK // 2, BLK // 2)))
         for c in to_near:
             c.start()
 
-        loads[3].wait()
-        wq_s[...] = wq3_s[...].reshape(wq_s.shape)
         pair.wait_recv()
         xh_s[...] = (xg_send[pl.ds(core * half, half), :].astype(F32) + xp_recv[...].astype(F32)).astype(BF16)
         swap = [remote(xh_s.at[pl.ds(0, quart)], xa_recv.at[0], x_ssem.at[1], x_rsem.at[1], x_peer),
@@ -154,6 +155,12 @@
         for c in swap:
             c.start()
 
+        @pl.when(has_far)
+        def _():
+            to_far[1].start()
+
+        loads[3].wait()
+        wq_s[...] = wq3_s[...].reshape(wq_s.shape)
         for h in range(heads):
             qh = (mm(x, wq_s[:, h * head:(h + 1) * head]) * head ** -0.5).astype(BF16)
             for b in range(n_blk):
@@ -272,8 +279,8 @@
 
             @pl.when(has_far)
             def _():
-                for c in to_far[::-1]:
-                    c.start()
+                to_far[2].start()
+                to_far[0].start()
 
             @pl.when(jnp.logical_not(has_far))
             def _():
@@ -311,6 +318,7 @@
 
         def inner_ready():
             wait_far(1)
+            wait_far(2)
 
         def outer_ready():
             wait_far(0)
@@ -500,7 +508,7 @@
             pltpu.VMEM((n_dev * slab, head), F32), pltpu.VMEM((n_dev, slab, head), F32),
             pltpu.VMEM((n_dev, 8, slab), F32), pltpu.VMEM((n_dev, 8, slab), F32),
             pltpu.VMEM((rows + per, dim), BF16), pltpu.VMEM((n_glob, dim), BF16), pltpu.VMEM((rows, heads * head), BF16),
-            dma((5,)), dma((6,)), dma((6,)), dma((4,)), dma((4,)), dma((n_dev,)), dma((n_dev,)), dma((n_dev,)), dma((n_dev,)),
+            dma((5,)), dma((6,)), dma((6,)), dma((5,)), dma((5,)), dma((n_dev,)), dma((n_dev,)), dma((n_dev,)), dma((n_dev,)),
             dma((n_dev,)), dma((n_dev,)), dma((w1.shape[1] // TILE,)), dma((w1.shape[1] // TILE,)), dma((PARTS + 1,)),
         ],
         compiler_params=pltpu.CompilerParams(collective_id=0, has_side_effects=True, vmem_limit_bytes=67043328),

time: 85 us -> 84 us (0.988)
  no operation moved by 1% of the time
where the time goes in v8:
time: 84 us; the launch traced here: 83.8 us
  Pallas kernels  83 us (99%)
    pallas_call x1, Pallas kernels, layer(): pl.pallas_call(functools.partial(layer_kernel, n_dev, heads, width), name...  78.5 us
    pallas_call x1, Pallas kernels, place(): pl.pallas_call(place_kernel, name='place', out_shape=(jax.ShapeDtypeStruc...  4.5 us

profile of v8, /device:TPU:0, one launch (start us, length us, event | category | flops | bytes accessed | tf_op | source)
XLA Modules:
  0.0 83.8 jit_solution(3798476441491464917)
XLA Ops:
  0.6 78.5 %layer.1 = (bf16[1024,1152]{1,0:T(8,128)(2,1)}, bf16[256,1152]{1,0:T(8,128)(2,1)}) custom-call(bf16[1024,1152]{1,0:T(8,128)(2,1)} %x_hbm.1, bf16[1152,4,256]{2,1,0:T(4,128)(2,1)} %wq_hbm.1, bf16[1152,256]{1,0:T(8,128)(2,1)} %bitcast.5, bf16[1152,256]{1,0:T(8,128)(2,1)} %bitcast.6, bf16[1024,1152]{1,0:T(8,128)(2,1)} %bitcast.4, bf16[1152,6912]{1,0:T(8,128)(2,1)} %w1_hbm.1, ...), custom_call_target="tpu_custom_call" | custom-call | tf_op jit(solution)/shard_map/layer/pallas_call | solution.py:497
  79.2 4.5 %place.1 = (bf16[1024,1152]{1,0:T(8,128)(2,1)}, bf16[256,1152]{1,0:T(8,128)(2,1)}) custom-call(bf16[1024,1152]{1,0:T(8,128)(2,1)} %get-tuple-element.4.ys_hbm, bf16[256,1152]{1,0:T(8,128)(2,1)} %get-tuple-element.5.yg_hbm, s32[1,256]{1,0:T(1,128)} %bitcast.8), custom_call_target="tpu_custom_call" | custom-call | tf_op jit(solution)/shard_map/place/pallas_call | solution.py:549

commit v9 on v8

--- a/solution.py
+++ b/solution.py
@@ -420,24 +420,24 @@
             lax.fori_loop(0, steps, step, 0)
             hid_s[r, :] = (acc_s[...] + mm(u_s[...], w2_s[n_tile - 1, TILE - BLK:, :])).astype(BF16)
 
-        def first(i, carry):
-            for c in w_copies(i):
-                c.wait()
-            chunks(slice(0, part), i, TILE // BLK)
-            return carry
-
-        run_part(slice(0, part), n_tile, first)
-        out_copy(0).start()
-        finish_global()
-
         def later(p, carry):
             r = pl.ds(pl.multiple_of(p * part, 16), part)
 
             def step(i, carry):
+                @pl.when(p == 0)
+                def _():
+                    for k in range(WIDE):
+                        for c in w_copies(i * WIDE + k):
+                            c.wait()
+
                 chunks(r, i * WIDE, WIDE * (TILE // BLK))
                 return carry
 
             run_part(r, n_tile // WIDE, step)
+
+            @pl.when(p == 0)
+            def _():
+                finish_global()
 
             @pl.when(p == PARTS - 2)
             def _():
@@ -445,14 +445,14 @@
                     yg_copy(k, lax.rem(me + k, n_dev), me).start()
                 yg_s[pl.ds(me * per, per), :] = hid_s[split:split + per, :]
 
-            for q in range(1, PARTS):
+            for q in range(PARTS):
                 @pl.when(p == q)
                 def _():
                     out_copy(q).start()
 
             return carry
 
-        lax.fori_loop(1, PARTS, later, 0)
+        lax.fori_loop(0, PARTS, later, 0)
 
     pl.run_scoped(
         front,

time: 84 us -> 84.1 us (level)
  no operation moved by 1% of the time
where the time goes in v9:
time: 84.1 us; the launch traced here: 83.9 us
  Pallas kernels  83.1 us (99%)
    pallas_call x1, Pallas kernels, layer(): pl.pallas_call(functools.partial(layer_kernel, n_dev, heads, width), name...  78.6 us
    pallas_call x1, Pallas kernels, place(): pl.pallas_call(place_kernel, name='place', out_shape=(jax.ShapeDtypeStruc...  4.5 us

profile of v9, /device:TPU:0, one launch (start us, length us, event | category | flops | bytes accessed | tf_op | source)
XLA Modules:
  0.0 83.9 jit_solution(6719494451091771439)
XLA Ops:
  0.6 78.6 %layer.1 = (bf16[1024,1152]{1,0:T(8,128)(2,1)}, bf16[256,1152]{1,0:T(8,128)(2,1)}) custom-call(bf16[1024,1152]{1,0:T(8,128)(2,1)} %x_hbm.1, bf16[1152,4,256]{2,1,0:T(4,128)(2,1)} %wq_hbm.1, bf16[1152,256]{1,0:T(8,128)(2,1)} %bitcast.5, bf16[1152,256]{1,0:T(8,128)(2,1)} %bitcast.6, bf16[1024,1152]{1,0:T(8,128)(2,1)} %bitcast.4, bf16[1152,6912]{1,0:T(8,128)(2,1)} %w1_hbm.1, ...), custom_call_target="tpu_custom_call" | custom-call | tf_op jit(solution)/shard_map/layer/pallas_call | solution.py:497
  79.3 4.5 %place.1 = (bf16[1024,1152]{1,0:T(8,128)(2,1)}, bf16[256,1152]{1,0:T(8,128)(2,1)}) custom-call(bf16[1024,1152]{1,0:T(8,128)(2,1)} %get-tuple-element.4.ys_hbm, bf16[256,1152]{1,0:T(8,128)(2,1)} %get-tuple-element.5.yg_hbm, s32[1,256]{1,0:T(1,128)} %bitcast.8), custom_call_target="tpu_custom_call" | custom-call | tf_op jit(solution)/shard_map/place/pallas_call | solution.py:549

commit v10 on v9

--- a/solution.py
+++ b/solution.py
@@ -423,14 +423,29 @@
         def later(p, carry):
             r = pl.ds(pl.multiple_of(p * part, 16), part)
 
+            def narrow(k, carry):
+                for c in w_copies(k):
+                    c.wait()
+                chunks(r, k, TILE // BLK)
+                return carry
+
             def step(i, carry):
-                @pl.when(p == 0)
+                fresh = (p == 0) & (i == 0)
+
+                @pl.when(fresh)
+                def _():
+                    lax.fori_loop(0, WIDE, narrow, 0)
+
+                @pl.when((p == 0) & (i > 0))
                 def _():
                     for k in range(WIDE):
                         for c in w_copies(i * WIDE + k):
                             c.wait()
 
-                chunks(r, i * WIDE, WIDE * (TILE // BLK))
+                @pl.when(jnp.logical_not(fresh))
+                def _():
+                    chunks(r, i * WIDE, WIDE * (TILE // BLK))
+
                 return carry
 
             run_part(r, n_tile // WIDE, step)

time: 84.1 us -> 83.7 us (level)
  no operation moved by 1% of the time
where the time goes in v10:
time: 83.7 us; the launch traced here: 83.5 us
  Pallas kernels  82.7 us (99%)
    pallas_call x1, Pallas kernels, layer(): pl.pallas_call(functools.partial(layer_kernel, n_dev, heads, width), name...  78.2 us
    pallas_call x1, Pallas kernels, place(): pl.pallas_call(place_kernel, name='place', out_shape=(jax.ShapeDtypeStruc...  4.5 us

profile of v10, /device:TPU:0, one launch (start us, length us, event | category | flops | bytes accessed | tf_op | source)
XLA Modules:
  0.0 83.5 jit_solution(3959162219957189682)
XLA Ops:
  0.6 78.2 %layer.1 = (bf16[1024,1152]{1,0:T(8,128)(2,1)}, bf16[256,1152]{1,0:T(8,128)(2,1)}) custom-call(bf16[1024,1152]{1,0:T(8,128)(2,1)} %x_hbm.1, bf16[1152,4,256]{2,1,0:T(4,128)(2,1)} %wq_hbm.1, bf16[1152,256]{1,0:T(8,128)(2,1)} %bitcast.5, bf16[1152,256]{1,0:T(8,128)(2,1)} %bitcast.6, bf16[1024,1152]{1,0:T(8,128)(2,1)} %bitcast.4, bf16[1152,6912]{1,0:T(8,128)(2,1)} %w1_hbm.1, ...), custom_call_target="tpu_custom_call" | custom-call | tf_op jit(solution)/shard_map/layer/pallas_call | solution.py:512
  78.8 4.5 %place.1 = (bf16[1024,1152]{1,0:T(8,128)(2,1)}, bf16[256,1152]{1,0:T(8,128)(2,1)}) custom-call(bf16[1024,1152]{1,0:T(8,128)(2,1)} %get-tuple-element.4.ys_hbm, bf16[256,1152]{1,0:T(8,128)(2,1)} %get-tuple-element.5.yg_hbm, s32[1,256]{1,0:T(1,128)} %bitcast.8), custom_call_target="tpu_custom_call" | custom-call | tf_op jit(solution)/shard_map/place/pallas_call | solution.py:564
